TPU v7x, 512 devices: a whole 4x4x16 slice. The times are simulated.
512 devices in a mesh: owner: 32 (over z, core), sub: 16 (over x, y).
Axes of the slice: x: 4, y: 4, z: 16, core: 2. Of those that a mesh axis runs over, the one named last changes fastest.
Arguments:
- residual: float32 [256, 73728], P('owner', 'sub'), may hold values from -6 to 6
- counts: int32 [32, 64], P('owner', 'sub'), may hold values from 1 to 36
- assembly: int32 [32, 64, 36, 2304], P('owner', 'sub'), may hold values from 0 to 1, as said below
- level_two: float32 [32, 2304, 2304], P('owner', 'sub'), as said below
- block_inverse: float32 [32, 2304, 144], P('owner', 'sub'), as said below
Outputs:
- corrections: float32 [256, 73728], P('owner', 'sub')
- level_residual: float32 [32, 2304, 256], P('owner', 'sub')
Inputs may be any that keep to these rules, and one draw needn't show every extreme that they name: `assembly`: every row of each [36, 2304] block holds exactly one 1; split the 2304 columns into 16 equal ranges and a group's positions into runs of 4: the 144 rows of one run (live or not) put at most 18 of their 1s into one range, and in every run some range gets exactly 18. `level_two`: each group's matrix is symmetric positive definite. `block_inverse`: each diagonal block is symmetric positive definite.
All inputs are finite; a program needn't handle non-finite values.
Results may differ from a plain program's by a relative error of at most 0.0003.
Values sent between devices are 32-bit elements; how exact they have to be, the bound alone decides.
A program may use at most 64 MiB of HBM per device.

v0:
```python
import math

import jax
import jax.numpy as jnp
from jax import lax
from jax.sharding import PartitionSpec as P

ITERS = 4


def in_one_piece(arrays, axis, split_dim, concat_dim, along):
    widths = [math.prod(a.shape[along:]) for a in arrays]
    both = jnp.concatenate(
        [a.reshape(*a.shape[:along], w) for a, w in zip(arrays, widths)], axis=along
    )
    whole = lax.all_to_all(both, axis, split_axis=split_dim, concat_axis=concat_dim, tiled=True)
    parts = jnp.split(whole, [sum(widths[:k]) for k in range(1, len(widths))], axis=along)
    return tuple((b.reshape(*whole.shape[:along], *a.shape[along:]) for a, b in zip(arrays, parts)))


def in_order(parts, dim):
    shape = list(parts.shape[1:])
    shape[dim] *= parts.shape[0]
    return jnp.moveaxis(parts, 0, dim).reshape(shape)


def copy_for_each(shard, axis):
    size = lax.axis_size(axis)
    return lax.all_to_all(
        jnp.broadcast_to(shard[None], (size, *shard.shape)), axis, 0, 0, tiled=True
    )


def collect(shard, axis, dim):
    return in_order(copy_for_each(shard, axis), dim)


def of_everyone(shard, axis):
    everything = copy_for_each(shard, axis)
    return jnp.sum(everything, axis=0)


def in_one(arrays, axis):
    ravelled, at, gathered = (jnp.concatenate([a.reshape(-1) for a in arrays]), 0, [])
    so_far = of_everyone(ravelled, axis)
    for a in arrays:
        gathered.append(so_far[at : at + a.size].reshape(a.shape))
        at += a.size
    return tuple(gathered)


def column_sum(left, right):
    return jnp.sum(left * right, axis=0)


def shards(residual, counts, assembly, level_two, block_inverse):
    highest = lax.Precision.HIGHEST
    rows_here = level_two.shape[1]
    width = level_two.shape[2]
    block = block_inverse.shape[2]
    slots = assembly.shape[1]
    prim = assembly.shape[2]
    rows_local = slots * prim
    local = lax.all_to_all(residual, "owner", split_axis=1, concat_axis=0, tiled=True)
    live = (lax.broadcasted_iota(jnp.int32, (slots, prim), 1) < counts[0][:, None]).astype(
        jnp.float32
    )
    live_flat = live.reshape(rows_local)
    nsub = lax.axis_size("sub")
    capacity = max(2 * rows_local // nsub, 1)
    total_slots = nsub * capacity
    flat = assembly[0].reshape(rows_local, width)
    target = jnp.sum(flat * lax.broadcasted_iota(jnp.int32, (rows_local, width), 1), axis=1)
    holder = target // rows_here
    offset = target - holder * rows_here
    same = holder[:, None] == holder[None, :]
    earlier = lax.broadcasted_iota(jnp.int32, (rows_local, rows_local), 0) > lax.broadcasted_iota(
        jnp.int32, (rows_local, rows_local), 1
    )
    rank = jnp.sum((same & earlier).astype(jnp.int32), axis=1)
    place = holder * capacity + rank
    pick = (place[:, None] == lax.broadcasted_iota(jnp.int32, (rows_local, total_slots), 1)).astype(
        jnp.float32
    )
    pick_live = pick * live_flat[:, None]
    send_vals = lax.dot_general(
        pick_live,
        local,
        (((0,), (1,)), ((), ())),
        precision=highest,
        preferred_element_type=jnp.float32,
    )
    used = jnp.sum(pick, axis=0)
    send_off = (
        jnp.dot(
            offset.astype(jnp.float32), pick, precision=highest, preferred_element_type=jnp.float32
        )
        + (1.0 - used) * rows_here
    )
    recv_vals, recv_off = in_one_piece((send_vals, send_off), "sub", 0, 0, 1)
    landing = (
        recv_off.astype(jnp.int32)[:, None]
        == lax.broadcasted_iota(jnp.int32, (total_slots, rows_here), 1)
    ).astype(jnp.float32)
    level_rhs = lax.dot_general(
        landing,
        recv_vals,
        (((0,), (0,)), ((), ())),
        precision=highest,
        preferred_element_type=jnp.float32,
    )
    matrix = level_two[0]
    inverse = block_inverse[0].reshape(rows_here // block, block, block)

    def precond(vector):
        shaped = vector.reshape(rows_here // block, block, vector.shape[1])
        return jnp.einsum("bij,bjr->bir", inverse, shaped, precision=highest).reshape(
            rows_here, vector.shape[1]
        )

    def apply_matrix(vector):
        return jnp.dot(
            matrix, collect(vector, "sub", 0), precision=highest, preferred_element_type=jnp.float32
        )

    def global_pair(resid, zvec, image):
        return in_one((column_sum(resid, zvec), column_sum(zvec, image)), "sub")

    resid = level_rhs
    zvec = precond(resid)
    image = apply_matrix(zvec)
    gamma, delta = global_pair(resid, zvec, image)
    alpha = gamma / delta
    direction, along = (zvec, image)
    solution = alpha * direction
    resid = resid - alpha * along
    for step in range(1, ITERS):
        zvec = precond(resid)
        image = apply_matrix(zvec)
        gamma_next, delta = global_pair(resid, zvec, image)
        ratio = gamma_next / gamma
        alpha = gamma_next / (delta - ratio * gamma_next / alpha)
        direction = zvec + ratio * direction
        along = image + ratio * along
        solution = solution + alpha * direction
        resid = resid - alpha * along
        gamma = gamma_next
    reply = jnp.dot(landing, solution, precision=highest, preferred_element_type=jnp.float32)
    returned = lax.all_to_all(reply, "sub", split_axis=0, concat_axis=0, tiled=True)
    gathered = lax.dot_general(
        returned,
        pick_live,
        (((0,), (1,)), ((), ())),
        precision=highest,
        preferred_element_type=jnp.float32,
    )
    corrections = lax.all_to_all(gathered, "owner", split_axis=0, concat_axis=1, tiled=True)
    return (corrections, resid[None])


def solution(mesh):
    in_specs = (
        P("owner", "sub"),
        P("owner", "sub"),
        P("owner", "sub", None, None),
        P("owner", "sub", None),
        P("owner", "sub", None),
    )
    out_specs = (P("owner", "sub"), P("owner", "sub", None))
    return jax.shard_map(shards, mesh=mesh, in_specs=in_specs, out_specs=out_specs, check_vma=False)
```

profile of v0, /device:TPU:1, one launch (start us, length us, event | category | flops | bytes accessed | tf_op | source)
XLA Modules:
  0.0 278.6 jit_solution(2256751314443811016)
XLA Ops:
  0.6 0.0 copy-start
  0.7 1.2 all_to_all.68
  1.9 0.8 copy.32
  2.8 16.7 %all-to-all-start = ((f32[8,32,144]{2,0,1:T(8,128)}), f32[8,32,144]{2,0,1:T(8,128)S(1)}, u32[]{:S(2)}, u32[]{:S(2)}) async-start(f32[8,32,144]{2,0,1:T(8,128)} %copy.32), calls=%async_computation | async-start | bytes 524288 | tf_op jit(solution)/shard_map/all_to_all | solution.py:64
  19.5 0.7 multiply_reduce_fusion
  20.2 0.1 copy.31
  20.3 0.1 reduce_sum.138
  20.4 0.2 convert_reduce_fusion.1
  20.6 0.1 fusion.67
  20.7 0.1 reshape.194
  20.8 0.3 convolution_reduce_fusion
  21.1 0.1 convert_reduce_fusion
  21.2 0.2 concatenate.24
  21.4 20.4 %all-to-all-done = f32[8,32,144]{2,0,1:T(8,128)S(1)} async-done(((f32[8,32,144]{2,0,1:T(8,128)}), f32[8,32,144]{2,0,1:T(8,128)S(1)}, u32[]{:S(2)}, u32[]{:S(2)}) %all-to-all-start) | async-done | bytes 147488 | tf_op jit(solution)/shard_map/all_to_all | solution.py:64
  41.8 0.5 fusion.22
  42.3 17.7 %all_to_all.100 = f32[16,18,257]{2,1,0:T(8,128)S(1)} all-to-all(f32[16,18,257]{2,1,0:T(8,128)S(1)} %pad_maximum_fusion), channel_id=1, replica_groups=mesh['owner'=32,'sub'=16] {'sub'}, dimensions={0} | all-to-all | bytes 592128 | tf_op jit(solution)/shard_map/all_to_all | solution.py:16
  60.0 0.1 all_to_all.73
  60.1 0.1 fusion.35
  60.2 0.6 fusion.25
  60.8 0.3 convolution_bitcast_fusion.3
  61.1 0.2 broadcast_in_dim.18
  61.3 31.8 %all_to_all.101 = f32[16,144,256]{2,1,0:T(8,128)S(1)} all-to-all(f32[16,144,256]{2,1,0:T(8,128)S(1)} %broadcast_in_dim.18), channel_id=1, replica_groups=mesh['owner'=32,'sub'=16] {'sub'}, dimensions={0} | all-to-all | bytes 4718592 | tf_op jit(solution)/shard_map/all_to_all | solution.py:29
  93.1 1.6 multiply_reduce_fusion.8
  94.7 10.1 %all_to_all.102 = f32[16,1,512]{2,1,0:T(1,128)S(1)} all-to-all(f32[16,1,512]{2,1,0:T(1,128)S(1)} %broadcast_in_dim.19), channel_id=1, replica_groups=mesh['owner'=32,'sub'=16] {'sub'}, dimensions={0} | all-to-all | bytes 65536 | tf_op jit(solution)/shard_map/all_to_all | solution.py:29
  104.9 0.3 convolution_bitcast_fusion.2
  105.2 0.2 broadcast_in_dim.20
  105.4 28.6 %all_to_all.103 = f32[16,144,256]{2,1,0:T(8,128)S(1)} all-to-all(f32[16,144,256]{2,1,0:T(8,128)S(1)} %broadcast_in_dim.20), channel_id=1, replica_groups=mesh['owner'=32,'sub'=16] {'sub'}, dimensions={0} | all-to-all | bytes 4718592 | tf_op jit(solution)/shard_map/all_to_all | solution.py:29
  134.0 1.6 multiply_reduce_fusion.6
  135.6 10.3 %all_to_all.104 = f32[16,1,512]{2,1,0:T(1,128)S(1)} all-to-all(f32[16,1,512]{2,1,0:T(1,128)S(1)} %broadcast_in_dim.21), channel_id=1, replica_groups=mesh['owner'=32,'sub'=16] {'sub'}, dimensions={0} | all-to-all | bytes 65536 | tf_op jit(solution)/shard_map/all_to_all | solution.py:29
  146.0 0.3 convolution_bitcast_fusion.1
  146.3 0.2 broadcast_in_dim.22
  146.5 26.1 %all_to_all.105 = f32[16,144,256]{2,1,0:T(8,128)S(1)} all-to-all(f32[16,144,256]{2,1,0:T(8,128)S(1)} %broadcast_in_dim.22), channel_id=1, replica_groups=mesh['owner'=32,'sub'=16] {'sub'}, dimensions={0} | all-to-all | bytes 4718592 | tf_op jit(solution)/shard_map/all_to_all | solution.py:29
  172.6 1.6 multiply_reduce_fusion.4
  174.2 11.0 %all_to_all.106 = f32[16,1,512]{2,1,0:T(1,128)S(1)} all-to-all(f32[16,1,512]{2,1,0:T(1,128)S(1)} %broadcast_in_dim.23), channel_id=1, replica_groups=mesh['owner'=32,'sub'=16] {'sub'}, dimensions={0} | all-to-all | bytes 65536 | tf_op jit(solution)/shard_map/all_to_all | solution.py:29
  185.3 0.3 convolution_bitcast_fusion
  185.6 0.2 broadcast_in_dim.24
  185.8 24.6 %all_to_all.107 = f32[16,144,256]{2,1,0:T(8,128)S(1)} all-to-all(f32[16,144,256]{2,1,0:T(8,128)S(1)} %broadcast_in_dim.24), channel_id=1, replica_groups=mesh['owner'=32,'sub'=16] {'sub'}, dimensions={0} | all-to-all | bytes 4718592 | tf_op jit(solution)/shard_map/all_to_all | solution.py:29
  210.4 1.6 multiply_reduce_fusion.2
  212.0 10.0 %all_to_all.108 = f32[16,1,512]{2,1,0:T(1,128)S(1)} all-to-all(f32[16,1,512]{2,1,0:T(1,128)S(1)} %broadcast_in_dim.25), channel_id=1, replica_groups=mesh['owner'=32,'sub'=16] {'sub'}, dimensions={0} | all-to-all | bytes 65536 | tf_op jit(solution)/shard_map/all_to_all | solution.py:29
  222.0 0.4 fusion.27
  222.5 11.0 %all_to_all.109 = f32[16,18,256]{2,1,0:T(8,128)S(1)} all-to-all(f32[16,18,256]{2,1,0:T(8,128)S(1)} %all_to_all.82), channel_id=1, replica_groups=mesh['owner'=32,'sub'=16] {'sub'}, dimensions={0} | all-to-all | bytes 589824 | tf_op jit(solution)/shard_map/all_to_all | solution.py:149
  233.5 0.2 copy.39
  233.6 1.4 fusion.20
  235.0 20.5 %all-to-all-start.11 = ((f32[32,8,144]{2,1,0:T(8,128)}), f32[32,8,144]{2,1,0:T(8,128)S(1)}, u32[]{:S(2)}, u32[]{:S(2)}) async-start(f32[32,8,144]{2,1,0:T(8,128)} %fusion.20), calls=%async_computation.11 | async-start | bytes 524288 | tf_op jit(solution)/shard_map/all_to_all | solution.py:157
  255.5 0.7 subtract_bitcast_fusion
  256.2 21.6 %all-to-all-done.11 = f32[32,8,144]{2,1,0:T(8,128)S(1)} async-done(((f32[32,8,144]{2,1,0:T(8,128)}), f32[32,8,144]{2,1,0:T(8,128)S(1)}, u32[]{:S(2)}, u32[]{:S(2)}) %all-to-all-start.11) | async-done | bytes 147488 | tf_op jit(solution)/shard_map/all_to_all | solution.py:157
  277.7 0.1 copy.40
  277.8 0.8 all_to_all.87
  (33 shorter events, 0.6 us)
Async XLA Ops:
  0.6 92.5 %copy-start = (f32[1,144,2304]{2,1,0:T(8,128)S(1)}, f32[1,144,2304]{2,1,0:T(8,128)}, u32[]{:S(2)}) copy-start(f32[1,144,2304]{2,1,0:T(8,128)} %param.8) | copy-start | bytes 3981316
  0.6 18.9 %copy-start.2 = (s32[1,4,36,2304]{3,1,2,0:T(4,128)S(1)}, s32[1,4,36,2304]{3,1,2,0:T(4,128)}, u32[]{:S(2)}) copy-start(s32[1,4,36,2304]{3,1,2,0:T(4,128)} %param.7) | copy-start | bytes 3981316
  0.7 20.0 %copy-start.3 = (s32[1,4]{1,0:T(1,128)S(1)}, s32[1,4]{1,0:T(1,128)}, u32[]{:S(2)}) copy-start(s32[1,4]{1,0:T(1,128)} %param.6) | copy-start | bytes 52
  2.8 39.0 %all-to-all-start = ((f32[8,32,144]{2,0,1:T(8,128)}), f32[8,32,144]{2,0,1:T(8,128)S(1)}, u32[]{:S(2)}, u32[]{:S(2)}) async-start(f32[8,32,144]{2,0,1:T(8,128)} %copy.32), calls=%async_computation | async-start | bytes 524288 | tf_op jit(solution)/shard_map/all_to_all | solution.py:64
  21.4 39.4 %copy-start.1 = (f32[1,144,144]{2,1,0:T(8,128)S(1)}, f32[1,144,144]{2,1,0:T(8,128)}, u32[]{:S(2)}) copy-start(f32[1,144,144]{2,1,0:T(8,128)} %param.9) | copy-start | bytes 248836
  235.0 42.7 %all-to-all-start.11 = ((f32[32,8,144]{2,1,0:T(8,128)}), f32[32,8,144]{2,1,0:T(8,128)S(1)}, u32[]{:S(2)}, u32[]{:S(2)}) async-start(f32[32,8,144]{2,1,0:T(8,128)} %fusion.20), calls=%async_computation.11 | async-start | bytes 524288 | tf_op jit(solution)/shard_map/all_to_all | solution.py:157
where the time goes:
time: 279 us
  blocking collectives  181 us (65%)
  waiting for transfers between devices  41.9 us (15%)
  starting transfers between devices  37.2 us (13%)
  matrix products  10.4 us (4%)
  local copies, waits for them, and re-layouts  4.74 us (2%)
    all_to_all x8, blocking collectives, copy_for_each(): lax.all_to_all(jnp.broadcast_to(shard[None], (size, *shard.shape)), axis,...  152 us
    all_to_all x1, waiting for transfers between devices, shards(): lax.all_to_all(gathered, 'owner', split_axis=0, concat_axis=1, tiled=True)  21.6 us
    all_to_all x1, starting transfers between devices, shards(): lax.all_to_all(gathered, 'owner', split_axis=0, concat_axis=1, tiled=True)  20.5 us
    all_to_all x1, waiting for transfers between devices, shards(): lax.all_to_all(residual, 'owner', split_axis=1, concat_axis=0, tiled=True)  20.4 us
    all_to_all x1, blocking collectives, in_one_piece(): lax.all_to_all(both, axis, split_axis=split_dim, concat_axis=concat_dim,...  17.7 us
    all_to_all x1, starting transfers between devices, shards(): lax.all_to_all(residual, 'owner', split_axis=1, concat_axis=0, tiled=True)  16.7 us
    all_to_all x1, blocking collectives, shards(): lax.all_to_all(reply, 'sub', split_axis=0, concat_axis=0, tiled=True)  11 us
    dot_general x4, matrix products, apply_matrix(): jnp.dot(matrix, collect(vector, 'sub', 0), precision=highest, preferred_e...  6.24 us
  transfers between devices with their start and end apart: 2, of which 2 were waited for; matrix products, arithmetic and copies ran while one was open for 1% of the time, Pallas kernels for 0%

commit v1 on v0

v1 whole, which is shorter than its diff:
```python
import functools

import jax
import jax.numpy as jnp
from jax import lax
from jax.experimental import pallas as pl
from jax.experimental.pallas import tpu as pltpu
from jax.sharding import PartitionSpec as P

ITERS = 4
F32 = jnp.float32
BF16 = jnp.bfloat16
OWN = 32
SUB = 16
SIDE = 4
BLK = 144
SLOT = 18
PRIM = 36
LANES = 128
HALF = 64
PACK = 2 * BLK
MSG = 40
VEC = PACK + 8
CUT = 152


def iota(shape, dim):
    return lax.broadcasted_iota(jnp.int32, shape, dim)


def dot(a, b):
    return jnp.dot(a, b, preferred_element_type=F32)


def dot_nt(a, b):
    return lax.dot_general(a, b, (((1,), (1,)), ((), ())), preferred_element_type=F32)


def dot_tn(a, b):
    return lax.dot_general(a, b, (((0,), (0,)), ((), ())), preferred_element_type=F32)


def split(x):
    hi = x.astype(BF16)
    return hi, (x - hi.astype(F32)).astype(BF16)


def half_swap(x):
    return pltpu.roll(x, HALF, 1)


def low_half(shape):
    return iota(shape, 1) < HALF


def block_transpose(t):
    away = iota((8, LANES), 0) - iota((8, LANES), 1) // 16
    out = t
    for shift in range(1, 8):
        moved = pltpu.roll(pltpu.roll(t, shift, 0), LANES - 16 * shift, 1)
        out = jnp.where((away & 7) == shift, moved, out)
    return out


def kernel(
    res_ref, cnt_ref, asm_ref, mat_ref, inv_ref,
    corr_ref, resid_ref,
    zmain, ztail, zmain_in, ztail_in,
    cmain, ctail, cmain_in, ctail_in,
    offs, offs_in, info,
    rows_in, inv_in, stack, mstack,
    vsend, vin, land, land_t, pick,
    gsend, gin, wide, ssend, sin,
    psend, pin, back, rbuf, rin, local,
    zs_m, zr_m, zs_t, zr_t, cs_m, cr_m, cs_t, cr_t,
    os, orr, ms, mr, ivs, ivr, vs, vr, gs, gr, ss, sr, ps, pr, rs, rr,
):
    owner = lax.axis_index("owner")
    sub = lax.axis_index("sub")
    core = lax.rem(owner, 2)
    sx, sy = sub // SIDE, lax.rem(sub, SIDE)
    a = sx * (1 - core) + sy * core
    c = sy * (1 - core) + sx * core

    def at(ra, rc):
        return (4 * ra + rc) * (1 - core) + (4 * rc + ra) * core

    def ring(v, step):
        return lax.rem(v + step + SIDE, SIDE)

    def rcopy(src, dst, ssem, rsem, dev):
        return pltpu.make_async_remote_copy(
            src_ref=src, dst_ref=dst, send_sem=ssem, recv_sem=rsem,
            device_id=dev, device_id_type=pl.DeviceIdType.MESH,
        )

    barrier = pltpu.get_barrier_semaphore()

    @pl.loop(1, OWN)
    def _(j):
        pl.semaphore_signal(barrier, inc=1, device_id=(lax.rem(owner + j, OWN), sub),
                            device_id_type=pl.DeviceIdType.MESH)

    @pl.loop(1, SUB)
    def _(j):
        pl.semaphore_signal(barrier, inc=1, device_id=(owner, lax.rem(sub + j, SUB)),
                            device_id_type=pl.DeviceIdType.MESH)

    lane = iota((8, LANES), 1)
    low = low_half((8, LANES))

    def tile(t):
        return res_ref[:, LANES * t:LANES * (t + 1)]

    for k in range(4):
        tails = None
        for j in range(8):
            g = 8 * k + j
            if j == 0:
                main = tile(g + k)
            else:
                main = pltpu.roll(
                    jnp.where(lane >= 16 * j, tile(g + k), tile(g + k + 1)), LANES - 16 * j, 1
                )
            zmain[g] = main
            nxt = tile(g + k + 1)
            tails = nxt if j == 0 else jnp.where(lane // 16 == j, nxt, tails)
        moved = block_transpose(tails)
        for j in range(8):
            ztail[8 * k + j] = moved[j:j + 1, :]

    col = iota((8, SUB * BLK), 1)
    holder_of = col // BLK
    which = jnp.where(iota((8, SUB * BLK), 0) == 0, col - holder_of * BLK, holder_of)
    which = which.astype(F32).astype(BF16)
    info[...] = jnp.zeros_like(info)
    for j in range(4):
        block = asm_ref[j].astype(F32).astype(BF16)
        info[:, PRIM * j:PRIM * (j + 1)] = dot_nt(which, block)
    place8 = info[...]
    inside = place8.astype(BF16)
    held = place8[1:2, :].astype(jnp.int32)
    dof = iota((1, 256), 1)
    which_sub = ((dof >= PRIM).astype(jnp.int32) + (dof >= 2 * PRIM).astype(jnp.int32)
                 + (dof >= 3 * PRIM).astype(jnp.int32))
    count = jnp.where(which_sub == 0, cnt_ref[0, 0], jnp.where(
        which_sub == 1, cnt_ref[0, 1], jnp.where(which_sub == 2, cnt_ref[0, 2], cnt_ref[0, 3])))
    live = ((dof - PRIM * which_sub) < count) & (dof < BLK)
    held = jnp.where(live, held, -1)
    hot = (held == iota((SUB, 256), 0)).astype(F32)
    upper = (iota((256, 256), 0) < iota((256, 256), 1)).astype(F32).astype(BF16)
    rank = jnp.sum(hot * dot(hot.astype(BF16), upper), axis=0, keepdims=True).astype(jnp.int32)
    hx, hy = held // SIDE, held & 3
    ha = hx * (1 - core) + hy * core
    hk = hy * (1 - core) + hx * core
    spot = ha * LANES + (hk // 2) * HALF + (hk & 1) * SLOT + rank
    spot = jnp.where(live, spot, -1)
    pick[...] = (iota((4 * LANES, 256), 0) == spot).astype(F32).astype(BF16)
    rows = dot_nt(inside, pick[...])
    for j in range(4):
        offs[j] = rows[0:1, LANES * j:LANES * (j + 1)]

    pl.semaphore_wait(barrier, OWN - 1 + SUB - 1)

    @pl.loop(1, OWN)
    def _(j):
        peer = lax.rem(owner + j, OWN)
        rcopy(zmain.at[peer], zmain_in.at[owner], zs_m.at[peer], zr_m.at[owner], (peer, sub)).start()
        rcopy(ztail.at[peer], ztail_in.at[owner], zs_t.at[peer], zr_t.at[owner], (peer, sub)).start()

    def off_copy(peer, pa):
        return rcopy(offs.at[pa], offs_in.at[sub], os.at[peer], orr.at[sub], (owner, peer))

    def group_of(peer):
        px, py = peer // SIDE, lax.rem(peer, SIDE)
        return px * (1 - core) + py * core, py * (1 - core) + px * core

    @pl.loop(1, SUB)
    def _(j):
        peer = lax.rem(sub + j, SUB)
        pa, _pc = group_of(peer)
        off_copy(peer, pa).start()

    nextc, prevc = ring(c, 1), ring(c, -1)
    oppc = ring(c, 2)
    c_right, c_left, c_opp = (owner, at(a, nextc)), (owner, at(a, prevc)), (owner, at(a, oppc))
    for n, dev in ((0, c_right), (1, c_left), (2, c_opp)):
        rcopy(inv_ref, inv_in.at[c], ivs.at[n], ivr.at[n], dev).start()

    top, bottom = pl.ds(0, BLK // 2), pl.ds(BLK // 2, BLK // 2)

    def mat_copy(n, slot, part, dev, src=None):
        source = mat_ref.at[part] if src is None else src
        return rcopy(source, rows_in.at[slot, part], ms.at[n], mr.at[n], dev)

    mat_copy(0, c, top, c_right).start()
    mat_copy(2, c, bottom, c_left).start()
    mat_copy(1, c, bottom, c_right).start()
    mat_copy(3, c, top, c_left).start()

    zmain_in[owner] = zmain[owner]
    ztail_in[owner] = ztail[owner]
    offs_in[sub] = offs[a]
    inv_in[c] = inv_ref[...]
    vin[:, MSG:HALF, :] = jnp.zeros((SUB, HALF - MSG, LANES), F32)
    back[...] = jnp.zeros_like(back)

    @pl.loop(1, SUB)
    def _(j):
        peer = lax.rem(sub + j, SUB)
        rcopy(offs.at[0], offs_in.at[peer], os.at[peer], orr.at[peer], (owner, peer)).wait_recv()

    lane1 = iota((1, LANES), 1)
    extra = jnp.where((lane1 & (HALF - 1)) >= SLOT, float(BLK), 0.0)
    for m in range(SUB // 2):
        one, two = offs_in[2 * m], offs_in[2 * m + 1]
        for h in range(2):
            if h == 0:
                row = jnp.where(lane1 < HALF, one, half_swap(two)) + extra
            else:
                row = jnp.where(lane1 < HALF, half_swap(one), two) + extra
            rowi = row.astype(jnp.int32)
            cols = pl.ds(LANES * m, LANES)
            land[h, :, cols] = (iota((PACK, LANES), 0) == rowi).astype(F32).astype(BF16)
            down = jnp.broadcast_to(row, (LANES, LANES)).T.astype(jnp.int32)
            for t, width in ((0, LANES), (1, LANES), (2, PACK - 2 * LANES)):
                hit = (down == iota((LANES, LANES), 1) + LANES * t).astype(F32).astype(BF16)
                land_t[h, cols, LANES * t:LANES * t + width] = hit[:, :width]

    def store_rows(slot, x):
        hi, lo = split(x)
        at_hi = pl.multiple_of(slot * BLK, 16)
        at_lo = pl.multiple_of((SIDE + slot) * BLK, 16)
        stack[pl.ds(at_hi, BLK), :] = hi
        stack[pl.ds(at_lo, BLK), :] = lo

    mat_copy(0, prevc, top, c_left).wait_recv()
    mat_copy(4, prevc, top, c_right, rows_in.at[prevc, top]).start()
    mat_copy(2, nextc, bottom, c_right).wait_recv()
    mat_copy(5, nextc, bottom, c_left, rows_in.at[nextc, bottom]).start()

    @pl.loop(1, OWN)
    def _(j):
        peer = lax.rem(owner + j, OWN)
        rcopy(zmain.at[peer], zmain_in.at[peer], zs_m.at[peer], zr_m.at[peer], (peer, sub)).wait_recv()
        rcopy(ztail.at[peer], ztail_in.at[peer], zs_t.at[peer], zr_t.at[peer], (peer, sub)).wait_recv()

    local[:, 0:LANES] = zmain_in[...].reshape(8 * OWN, LANES)
    for k in range(4):
        moved = block_transpose(ztail_in[8 * k:8 * (k + 1)].reshape(8, LANES))
        for j in range(8):
            src = 8 * k + j
            local[8 * src:8 * (src + 1), LANES:] = moved if j == 0 else pltpu.roll(
                moved, LANES - 16 * j, 1)
    loc_hi, loc_lo = split(local[...])
    vals = dot_nt(pick[...], loc_hi) + dot_nt(pick[...], loc_lo)
    low_msg = low_half((MSG, LANES))
    for ra in range(4):
        for t in range(2):
            first = vals[LANES * ra:LANES * ra + MSG, LANES * t:LANES * (t + 1)]
            second = vals[LANES * ra + HALF:LANES * ra + HALF + MSG, LANES * t:LANES * (t + 1)]
            vsend[4 * ra + 2 * t] = jnp.where(low_msg, first, half_swap(second))
            vsend[4 * ra + 2 * t + 1] = jnp.where(low_msg, half_swap(first), second)
    body = pl.ds(0, MSG)

    @pl.loop(1, SUB)
    def _(j):
        peer = lax.rem(sub + j, SUB)
        pa, pc = group_of(peer)
        rcopy(vsend.at[4 * pa + pc], vin.at[sub, body], vs.at[peer], vr.at[sub], (owner, peer)).start()

    vin[sub, body] = vsend[4 * a + c]
    store_rows(c, mat_ref[...])

    for n, slot in ((0, prevc), (1, nextc), (2, oppc)):
        rcopy(inv_ref, inv_in.at[slot], ivs.at[n], ivr.at[n], c_right).wait_recv()
    for k in range(4):
        hi, lo = split(inv_in[k])
        where_to = 2 * (k // 2) * BLK
        mstack[k % 2, where_to:where_to + BLK, :] = hi
        mstack[k % 2, where_to + BLK:where_to + 2 * BLK, :] = lo

    @pl.loop(1, SUB)
    def _(j):
        peer = lax.rem(sub + j, SUB)
        rcopy(vsend.at[0], vin.at[peer, body], vs.at[peer], vr.at[peer], (owner, peer)).wait_recv()

    low_pack = low_half((PACK, LANES))
    low_blk = low_half((BLK, LANES))

    def side_by_side(x):
        hi, lo = split(x)
        return jnp.concatenate([hi, lo], axis=1)

    def fold(x):
        return x[:, :LANES] + x[:, LANES:]

    values = side_by_side(vin[...].reshape(SUB * HALF, LANES))
    r = jnp.where(low_pack, fold(dot(land[0], values)), fold(dot(land[1], values)))

    def precond(v):
        out = []
        for kk in range(2):
            got = dot(mstack[kk], side_by_side(v[kk * BLK:(kk + 1) * BLK]))
            got = fold(got)
            out.append(jnp.where(low_blk, got[:BLK] + got[BLK:2 * BLK],
                                 got[2 * BLK:3 * BLK] + got[3 * BLK:]))
        return jnp.concatenate(out, axis=0)

    nexta, preva, oppa = ring(a, 1), ring(a, -1), ring(a, 2)
    a_right, a_left, a_opp = (owner, at(nexta, c)), (owner, at(preva, c)), (owner, at(oppa, c))
    head, rest = pl.ds(0, CUT), pl.ds(CUT, VEC - CUT)

    def vec_copy(it, n, slot, part, dev, forward=False):
        source = gin.at[it, slot, part] if forward else gsend.at[it, part]
        return rcopy(source, gin.at[it, slot, part], gs.at[it, n], gr.at[it, n], dev)

    def widen(ra, x):
        hi = x.astype(BF16).astype(F32)
        lo = x - hi
        first = jnp.where(low_pack, hi, half_swap(lo)).astype(BF16)
        second = jnp.where(low_pack, half_swap(hi), lo).astype(BF16)
        for k in range(4):
            piece = (first if k < 2 else second)[(k % 2) * BLK:(k % 2 + 1) * BLK]
            wide[pl.ds(pl.multiple_of(at(ra, k) * BLK, 16), BLK), :] = piece

    def gather_start(it, v, sums):
        gsend[it, 0:PACK] = v
        gsend[it, PACK:VEC] = sums
        vec_copy(it, 0, a, head, a_right).start()
        vec_copy(it, 2, a, rest, a_left).start()
        vec_copy(it, 1, a, rest, a_right).start()
        vec_copy(it, 3, a, head, a_left).start()
        widen(a, v)

    def gather_pass(it):
        vec_copy(it, 0, preva, head, a_left).wait_recv()
        vec_copy(it, 4, preva, head, a_right, True).start()
        vec_copy(it, 2, nexta, rest, a_right).wait_recv()
        vec_copy(it, 5, nexta, rest, a_left, True).start()
        vec_copy(it, 1, preva, rest, a_left).wait_recv()
        widen(preva, gin[it, preva, 0:PACK])
        vec_copy(it, 3, nexta, head, a_right).wait_recv()
        widen(nexta, gin[it, nexta, 0:PACK])

    def gather_end(it, sums):
        vec_copy(it, 4, oppa, head, a_right).wait_recv()
        vec_copy(it, 5, oppa, rest, a_left).wait_recv()
        widen(oppa, gin[it, oppa, 0:PACK])
        total = sums
        for ra in (preva, nexta, oppa):
            total = total + gin[it, ra, PACK:VEC]
        return total

    def product():
        got = dot(stack[...], wide[...])
        got = got[:SIDE * BLK] + got[SIDE * BLK:]
        got = got + half_swap(got)
        return jnp.where(low_pack, got[:PACK], got[PACK:])

    def column_sum(x, y):
        s = jnp.sum(x * y, axis=0, keepdims=True)
        return s + half_swap(s)

    row8 = iota((8, LANES), 0)

    def partial_sums(r, u, w):
        one, two = column_sum(r, u), column_sum(w, u)
        return jnp.where(row8 == 0, one, jnp.where(row8 == 1, two, 0.0))

    u = precond(r)
    nothing = jnp.zeros((8, LANES), F32)
    gather_start(0, u, nothing)
    gather_pass(0)

    mat_copy(1, prevc, bottom, c_left).wait_recv()
    store_rows(prevc, rows_in[prevc])
    mat_copy(3, nextc, top, c_right).wait_recv()
    store_rows(nextc, rows_in[nextc])
    mat_copy(4, oppc, top, c_right).wait_recv()
    mat_copy(5, oppc, bottom, c_left).wait_recv()
    store_rows(oppc, rows_in[oppc])

    gather_end(0, nothing)
    w = product()

    gamma = alpha = None
    x = p = s = q = z = None
    for it in range(1, ITERS):
        sums = partial_sums(r, u, w)
        m = precond(w)
        gather_start(it, m, sums)
        gather_pass(it)
        total = gather_end(it, sums)
        n = product()
        gamma_new, delta = total[0:1], total[1:2]
        if it == 1:
            alpha = gamma_new / delta
            z, q, s, p = n, m, w, u
            x = alpha * p
        else:
            beta = gamma_new / gamma
            alpha = gamma_new / (delta - beta * gamma_new / alpha)
            z, q, s, p = n + beta * z, m + beta * q, w + beta * s, u + beta * p
            x = x + alpha * p
        gamma = gamma_new
        r = r - alpha * s
        u = u - alpha * q
        w = w - alpha * z

    sums = partial_sums(r, u, w)
    ssend[...] = sums
    for n_, dev in ((0, a_right), (1, a_left), (2, a_opp)):
        rcopy(ssend, sin.at[n_], ss.at[n_], sr.at[n_], dev).start()
    total = sums
    for n_ in range(3):
        rcopy(ssend, sin.at[n_], ss.at[n_], sr.at[n_], a_right).wait_recv()
        total = total + sin[n_]
    gamma_new, delta = total[0:1], total[1:2]
    beta = gamma_new / gamma
    alpha = gamma_new / (delta - beta * gamma_new / alpha)
    s, p = w + beta * s, u + beta * p
    x = x + alpha * p
    r = r - alpha * s

    xs = side_by_side(x)
    low_slots = low_half((SUB * HALF, LANES))
    reply = jnp.where(low_slots, fold(dot(land_t[0], xs)), fold(dot(land_t[1], xs)))
    psend[...] = reply.reshape(SUB, HALF, LANES)
    mine = 4 * a + c

    @pl.loop(1, SUB)
    def _(j):
        peer = lax.rem(sub + j, SUB)
        rcopy(psend.at[peer, body], pin.at[mine], ps.at[peer], pr.at[mine], (owner, peer)).start()

    pin[mine] = psend[sub, body]

    rbuf[...] = r
    for n_, slot, dev in ((0, nextc, c_right), (1, prevc, c_left), (2, oppc, c_opp)):
        source = rbuf.at[pl.ds(pl.multiple_of(lax.rem(slot, 2) * BLK, 8), BLK)]
        rcopy(source, rin.at[c], rs.at[n_], rr.at[n_], dev).start()
    rin[c] = rbuf[pl.ds(pl.multiple_of(lax.rem(c, 2) * BLK, 8), BLK)]

    @pl.loop(1, SUB)
    def _(j):
        peer = lax.rem(sub + j, SUB)
        pa, pc = group_of(peer)
        slot = 4 * pa + pc
        rcopy(psend.at[peer, body], pin.at[slot], ps.at[peer], pr.at[slot], (owner, peer)).wait_recv()

    for ra in range(4):
        for t in range(2):
            one, two = pin[4 * ra + 2 * t], pin[4 * ra + 2 * t + 1]
            cols = slice(LANES * t, LANES * (t + 1))
            back[LANES * ra:LANES * ra + MSG, cols] = jnp.where(low_msg, one, half_swap(two))
            back[LANES * ra + HALF:LANES * ra + HALF + MSG, cols] = jnp.where(
                low_msg, half_swap(one), two)
    back_hi, back_lo = split(back[...])
    mine_back = dot_tn(back_hi, pick[...]) + dot_tn(back_lo, pick[...])
    cmain[...] = mine_back[:, :LANES].reshape(OWN, 8, LANES)
    for k in range(4):
        tails = None
        for j in range(8):
            src = 8 * k + j
            piece = mine_back[8 * src:8 * (src + 1), LANES:]
            tails = piece if j == 0 else tails + pltpu.roll(piece, 16 * j, 1)
        moved = block_transpose(tails)
        for j in range(8):
            ctail[8 * k + j] = moved[j:j + 1, :]

    @pl.loop(1, OWN)
    def _(j):
        peer = lax.rem(owner + j, OWN)
        rcopy(cmain.at[peer], cmain_in.at[owner], cs_m.at[peer], cr_m.at[owner], (peer, sub)).start()
        rcopy(ctail.at[peer], ctail_in.at[owner], cs_t.at[peer], cr_t.at[owner], (peer, sub)).start()

    cmain_in[owner] = cmain[owner]
    ctail_in[owner] = ctail[owner]

    for n_, slot in ((0, prevc), (1, nextc), (2, oppc)):
        rcopy(rbuf.at[pl.ds(0, BLK)], rin.at[slot], rs.at[n_], rr.at[n_], c_right).wait_recv()
    for t in range(2):
        one, two = rin[2 * t], rin[2 * t + 1]
        upper_half = jnp.where(low_blk, half_swap(one), two)
        lower_half = jnp.where(low_blk, one, half_swap(two))
        resid_ref[:, LANES * t:LANES * (t + 1)] = jnp.where(c < 2, lower_half, upper_half)

    for n_ in range(6):
        mat_copy(n_, c, top, c_right).wait_send()
        for it in range(ITERS):
            part = head if n_ in (0, 3, 4) else rest
            vec_copy(it, n_, a, part, a_right).wait_send()
    for n_ in range(3):
        rcopy(inv_ref, inv_in.at[c], ivs.at[n_], ivr.at[n_], c_right).wait_send()
        rcopy(ssend, sin.at[n_], ss.at[n_], sr.at[n_], a_right).wait_send()
        rcopy(rbuf.at[pl.ds(0, BLK)], rin.at[c], rs.at[n_], rr.at[n_], c_right).wait_send()

    @pl.loop(1, SUB)
    def _(j):
        peer = lax.rem(sub + j, SUB)
        rcopy(offs.at[0], offs_in.at[peer], os.at[peer], orr.at[peer], (owner, peer)).wait_send()
        rcopy(vsend.at[0], vin.at[peer, body], vs.at[peer], vr.at[peer], (owner, peer)).wait_send()
        rcopy(psend.at[peer, body], pin.at[peer], ps.at[peer], pr.at[peer], (owner, peer)).wait_send()

    @pl.loop(1, OWN)
    def _(j):
        peer = lax.rem(owner + j, OWN)
        rcopy(zmain.at[peer], zmain_in.at[peer], zs_m.at[peer], zr_m.at[peer], (peer, sub)).wait_send()
        rcopy(ztail.at[peer], ztail_in.at[peer], zs_t.at[peer], zr_t.at[peer], (peer, sub)).wait_send()
        rcopy(cmain.at[peer], cmain_in.at[peer], cs_m.at[peer], cr_m.at[peer], (peer, sub)).wait_recv()
        rcopy(ctail.at[peer], ctail_in.at[peer], cs_t.at[peer], cr_t.at[peer], (peer, sub)).wait_recv()

    @pl.loop(1, OWN)
    def _(j):
        peer = lax.rem(owner + j, OWN)
        rcopy(cmain.at[peer], cmain_in.at[peer], cs_m.at[peer], cr_m.at[peer], (peer, sub)).wait_send()
        rcopy(ctail.at[peer], ctail_in.at[peer], cs_t.at[peer], cr_t.at[peer], (peer, sub)).wait_send()

    for k in range(4):
        tails = block_transpose(ctail_in[8 * k:8 * (k + 1)].reshape(8, LANES))
        turned = [
            cmain_in[8 * k + j] if j == 0 else pltpu.roll(cmain_in[8 * k + j], 16 * j, 1)
            for j in range(8)
        ]
        for m in range(9):
            if m == 0:
                value = turned[0]
            else:
                value = jnp.where(lane < 16 * m, tails, turned[m]) if m < 8 else tails
                value = jnp.where(lane < 16 * (m - 1), turned[m - 1], value)
            where_to = LANES * (9 * k + m)
            corr_ref[:, where_to:where_to + LANES] = value


def shards(residual, counts, assembly, level_two, block_inverse):
    vmem = pl.BlockSpec(memory_space=pltpu.VMEM)
    smem = pl.BlockSpec(memory_space=pltpu.SMEM)
    anywhere = pl.BlockSpec(memory_space=pl.ANY)
    V = pltpu.VMEM
    dma = pltpu.SemaphoreType.DMA
    scratch = [
        V((OWN, 8, LANES), F32), V((OWN, 1, LANES), F32),
        V((OWN, 8, LANES), F32), V((OWN, 1, LANES), F32),
        V((OWN, 8, LANES), F32), V((OWN, 1, LANES), F32),
        V((OWN, 8, LANES), F32), V((OWN, 1, LANES), F32),
        V((SIDE, 1, LANES), F32), V((SUB, 1, LANES), F32), V((8, 256), F32),
        V((SIDE, BLK, SUB * BLK), F32), V((SIDE, BLK, BLK), F32),
        V((2 * SIDE * BLK, SUB * BLK), BF16), V((2, SIDE * BLK, BLK), BF16),
        V((SUB, MSG, LANES), F32), V((SUB, HALF, LANES), F32),
        V((2, PACK, SUB * HALF), BF16), V((2, SUB * HALF, PACK), BF16), V((4 * LANES, 256), BF16),
        V((ITERS, VEC, LANES), F32), V((ITERS, SIDE, VEC, LANES), F32),
        V((SUB * BLK, LANES), BF16), V((8, LANES), F32), V((3, 8, LANES), F32),
        V((SUB, HALF, LANES), F32), V((SUB, MSG, LANES), F32), V((4 * LANES, 256), F32),
        V((PACK, LANES), F32), V((SIDE, BLK, LANES), F32), V((256, 256), F32),
        dma((OWN,)), dma((OWN,)), dma((OWN,)), dma((OWN,)),
        dma((OWN,)), dma((OWN,)), dma((OWN,)), dma((OWN,)),
        dma((SUB,)), dma((SUB,)), dma((6,)), dma((6,)), dma((3,)), dma((3,)),
        dma((SUB,)), dma((SUB,)), dma((ITERS, 6)), dma((ITERS, 6)), dma((3,)), dma((3,)),
        dma((SUB,)), dma((SUB,)), dma((3,)), dma((3,)),
    ]
    corr, resid = pl.pallas_call(
        kernel,
        out_shape=(
            jax.ShapeDtypeStruct(residual.shape, F32),
            jax.ShapeDtypeStruct((BLK, 8 * OWN), F32),
        ),
        in_specs=[vmem, smem, vmem, vmem, vmem],
        out_specs=(vmem, vmem),
        scratch_shapes=scratch,
        compiler_params=pltpu.CompilerParams(
            collective_id=0, has_side_effects=True, vmem_limit_bytes=56 * 1024 * 1024
        ),
    )(residual, counts, assembly[0], level_two[0], block_inverse[0])
    return corr, resid[None]


def solution(mesh):
    in_specs = (
        P("owner", "sub"),
        P("owner", "sub"),
        P("owner", "sub", None, None),
        P("owner", "sub", None),
        P("owner", "sub", None),
    )
    out_specs = (P("owner", "sub"), P("owner", "sub", None))
    return jax.shard_map(shards, mesh=mesh, in_specs=in_specs, out_specs=out_specs, check_vma=False)
```

time: 279 us -> 127 us (0.46)
  blocking collectives: 181 us -> 0 us
  Pallas kernels: 0 us -> 120 us
  waiting for transfers between devices: 41.9 us -> 0 us
  starting transfers between devices: 37.2 us -> 0 us
  matrix products: 10.4 us -> 0 us
    all_to_all x10 -> x0, blocking collectives: 181 us -> none  [the longest x8 152 us: copy_for_each(): lax.all_to_all(jnp.broadcast_to(shard[None], (size, *shard.shape)), axis,...]
    pallas_call x0 -> x1, Pallas kernels: none -> 120 us  [shards(): pl.pallas_call(kernel, out_shape=(jax.ShapeDtypeStruct(residual.shape, F3...]
    all_to_all x2 -> x0, waiting for transfers between devices: 41.9 us -> none  [the longest x1 21.6 us: shards(): lax.all_to_all(gathered, 'owner', split_axis=0, concat_axis=1, tiled=True)]
    all_to_all x2 -> x0, starting transfers between devices: 37.2 us -> none  [the longest x1 20.5 us: shards(): lax.all_to_all(gathered, 'owner', split_axis=0, concat_axis=1, tiled=True)]
    dot_general x13 -> x0, matrix products: 10.4 us -> none  [the longest x4 6.24 us: apply_matrix(): jnp.dot(matrix, collect(vector, 'sub', 0), precision=highest, preferred_e...]
    unnamed x8 -> x3, local copies, waits for them, and re-layouts: 0.02 us -> 5.89 us
    all_to_all x7 -> x0, local copies, waits for them, and re-layouts: 3.13 us -> none  [the longest x2 2.08 us: shards(): lax.all_to_all(residual, 'owner', split_axis=1, concat_axis=0, tiled=True)]
  transfers between devices with their start and end apart: 2 -> 0, of which waited for: 2 -> 0; matrix products, arithmetic and copies ran while one was open for 1% -> 0% of each run, Pallas kernels for 0% -> 0%
where the time goes in v1:
time: 127 us
  Pallas kernels  120 us (94%)
  local copies, waits for them, and re-layouts  5.89 us (5%)
    pallas_call x1, Pallas kernels, shards(): pl.pallas_call(kernel, out_shape=(jax.ShapeDtypeStruct(residual.shape, F3...  120 us
    unnamed x3, local copies, waits for them, and re-layouts  5.89 us

profile of v1, /device:TPU:1, one launch (start us, length us, event | category | flops | bytes accessed | tf_op | source)
XLA Modules:
  0.0 127.0 jit_solution(12243687735116742284)
XLA Ops:
  0.6 2.7 %copy.9 = s32[1,4,36,2304]{3,2,1,0:T(8,128)} copy(s32[1,4,36,2304]{3,1,2,0:T(4,128)} %param.7) | data formatting | bytes 2654208 | tf_op args[2]
  3.4 120.5 %shard_map.68 = (f32[8,4608]{1,0:T(8,128)}, f32[144,256]{1,0:T(8,128)}) custom-call(f32[8,4608]{1,0:T(8,128)} %res_ref.1, s32[1,4]{1,0:T(1,128)} %cnt_ref.1, s32[4,36,2304]{2,1,0:T(8,128)} %bitcast.6, f32[144,2304]{1,0:T(8,128)} %bitcast.7, f32[144,144]{1,0:T(8,128)} %bitcast.8), custom_call_target="tpu_custom_call" | custom-call | tf_op jit(solution)/shard_map/pallas_call | solution.py:562
  123.8 1.6 %copy.12 = f32[8,4608]{1,0:T(8,128)} copy(f32[8,4608]{1,0:T(8,128)} %get-tuple-element.8) | data formatting | bytes 294912
  125.4 1.6 %copy.13 = f32[1,144,256]{2,1,0:T(8,128)} copy(f32[1,144,256]{2,1,0:T(8,128)} %bitcast.9) | data formatting | bytes 294912

commit v2 on v1

--- a/solution.py
+++ b/solution.py
@@ -21,6 +21,7 @@
 PACK = 2 * BLK
 MSG = 40
 VEC = PACK + 8
+TAIL = 24
 CUT = 152
 
 
@@ -63,15 +64,17 @@
 
 
 def kernel(
-    res_ref, cnt_ref, asm_ref, mat_ref, inv_ref,
+    cnt_ref, res_hbm, asm_hbm, mat_hbm, inv_hbm,
     corr_ref, resid_ref,
+    res_ref, asm_ref, inv_ref, inv_out,
     zmain, ztail, zmain_in, ztail_in,
     cmain, ctail, cmain_in, ctail_in,
     offs, offs_in, info,
-    rows_in, inv_in, stack, mstack,
+    rows_in, inv_in, inv_full, stack, mstack,
     vsend, vin, land, land_t, pick,
     gsend, gin, wide, ssend, sin,
-    psend, pin, back, rbuf, rin, local,
+    psend, pin, back, rbuf, rin, local, partial,
+    loads,
     zs_m, zr_m, zs_t, zr_t, cs_m, cr_m, cs_t, cr_t,
     os, orr, ms, mr, ivs, ivr, vs, vr, gs, gr, ss, sr, ps, pr, rs, rr,
 ):
@@ -106,8 +109,19 @@
         pl.semaphore_signal(barrier, inc=1, device_id=(owner, lax.rem(sub + j, SUB)),
                             device_id_type=pl.DeviceIdType.MESH)
 
+    fetches = [
+        pltpu.make_async_copy(res_hbm, res_ref, loads.at[0]),
+        pltpu.make_async_copy(asm_hbm, asm_ref, loads.at[1]),
+        pltpu.make_async_copy(inv_hbm, inv_ref, loads.at[2]),
+        pltpu.make_async_copy(mat_hbm, rows_in.at[c], loads.at[3]),
+    ]
+    for fetch in fetches:
+        fetch.start()
+
     lane = iota((8, LANES), 1)
     low = low_half((8, LANES))
+
+    fetches[0].wait()
 
     def tile(t):
         return res_ref[:, LANES * t:LANES * (t + 1)]
@@ -129,13 +143,20 @@
         for j in range(8):
             ztail[8 * k + j] = moved[j:j + 1, :]
 
+    fetches[2].wait()
+    inv_out[0:BLK] = inv_ref[:, 0:LANES]
+    inv_out[BLK:] = jnp.zeros((TAIL, LANES), F32)
+    for g in range(BLK // TAIL):
+        inv_out[BLK:, 16 * g:16 * (g + 1)] = inv_ref[TAIL * g:TAIL * (g + 1), LANES:BLK]
+
+    fetches[1].wait()
     col = iota((8, SUB * BLK), 1)
     holder_of = col // BLK
     which = jnp.where(iota((8, SUB * BLK), 0) == 0, col - holder_of * BLK, holder_of)
     which = which.astype(F32).astype(BF16)
     info[...] = jnp.zeros_like(info)
     for j in range(4):
-        block = asm_ref[j].astype(F32).astype(BF16)
+        block = asm_ref[:, j, :].astype(F32).astype(BF16)
         info[:, PRIM * j:PRIM * (j + 1)] = dot_nt(which, block)
     place8 = info[...]
     inside = place8.astype(BF16)
@@ -160,6 +181,8 @@
     for j in range(4):
         offs[j] = rows[0:1, LANES * j:LANES * (j + 1)]
 
+    fetches[3].wait()
+
     pl.semaphore_wait(barrier, OWN - 1 + SUB - 1)
 
     @pl.loop(1, OWN)
@@ -184,60 +207,60 @@
     nextc, prevc = ring(c, 1), ring(c, -1)
     oppc = ring(c, 2)
     c_right, c_left, c_opp = (owner, at(a, nextc)), (owner, at(a, prevc)), (owner, at(a, oppc))
-    for n, dev in ((0, c_right), (1, c_left), (2, c_opp)):
-        rcopy(inv_ref, inv_in.at[c], ivs.at[n], ivr.at[n], dev).start()
-
     top, bottom = pl.ds(0, BLK // 2), pl.ds(BLK // 2, BLK // 2)
 
-    def mat_copy(n, slot, part, dev, src=None):
-        source = mat_ref.at[part] if src is None else src
-        return rcopy(source, rows_in.at[slot, part], ms.at[n], mr.at[n], dev)
+    def mat_copy(n, slot, part, dev):
+        piece = rows_in.at[slot, part]
+        return rcopy(piece, piece, ms.at[n], mr.at[n], dev)
+
+    def inv_copy(n, slot, dev):
+        return rcopy(inv_out, inv_in.at[slot], ivs.at[n], ivr.at[n], dev)
 
     mat_copy(0, c, top, c_right).start()
     mat_copy(2, c, bottom, c_left).start()
     mat_copy(1, c, bottom, c_right).start()
     mat_copy(3, c, top, c_left).start()
+    for n, dev in ((0, c_right), (1, c_left), (2, c_opp)):
+        inv_copy(n, c, dev).start()
 
     zmain_in[owner] = zmain[owner]
     ztail_in[owner] = ztail[owner]
     offs_in[sub] = offs[a]
-    inv_in[c] = inv_ref[...]
+    inv_in[c] = inv_out[...]
     vin[:, MSG:HALF, :] = jnp.zeros((SUB, HALF - MSG, LANES), F32)
     back[...] = jnp.zeros_like(back)
 
-    @pl.loop(1, SUB)
-    def _(j):
-        peer = lax.rem(sub + j, SUB)
-        rcopy(offs.at[0], offs_in.at[peer], os.at[peer], orr.at[peer], (owner, peer)).wait_recv()
-
-    lane1 = iota((1, LANES), 1)
-    extra = jnp.where((lane1 & (HALF - 1)) >= SLOT, float(BLK), 0.0)
-    for m in range(SUB // 2):
-        one, two = offs_in[2 * m], offs_in[2 * m + 1]
-        for h in range(2):
-            if h == 0:
-                row = jnp.where(lane1 < HALF, one, half_swap(two)) + extra
-            else:
-                row = jnp.where(lane1 < HALF, half_swap(one), two) + extra
-            rowi = row.astype(jnp.int32)
-            cols = pl.ds(LANES * m, LANES)
-            land[h, :, cols] = (iota((PACK, LANES), 0) == rowi).astype(F32).astype(BF16)
-            down = jnp.broadcast_to(row, (LANES, LANES)).T.astype(jnp.int32)
-            for t, width in ((0, LANES), (1, LANES), (2, PACK - 2 * LANES)):
-                hit = (down == iota((LANES, LANES), 1) + LANES * t).astype(F32).astype(BF16)
-                land_t[h, cols, LANES * t:LANES * t + width] = hit[:, :width]
-
-    def store_rows(slot, x):
-        hi, lo = split(x)
-        at_hi = pl.multiple_of(slot * BLK, 16)
-        at_lo = pl.multiple_of((SIDE + slot) * BLK, 16)
-        stack[pl.ds(at_hi, BLK), :] = hi
-        stack[pl.ds(at_lo, BLK), :] = lo
-
-    mat_copy(0, prevc, top, c_left).wait_recv()
-    mat_copy(4, prevc, top, c_right, rows_in.at[prevc, top]).start()
-    mat_copy(2, nextc, bottom, c_right).wait_recv()
-    mat_copy(5, nextc, bottom, c_left, rows_in.at[nextc, bottom]).start()
+    def store_rows(k):
+        at_hi = pl.multiple_of(k * BLK, 16)
+        at_lo = pl.multiple_of((SIDE + k) * BLK, 16)
+        lanes = iota((BLK, LANES), 1)
+
+        @pl.loop(0, SIDE)
+        def _(d):
+            ra = ring(a, d)
+
+            def window(t, kk):
+                start = LANES * t + BLK * (at(ra, kk) - kk)
+                first, shift = start // LANES, lax.rem(start, LANES)
+                after = jnp.minimum(first + 1, SUB * BLK // LANES - 1)
+                one = rows_in[k, :, pl.ds(pl.multiple_of(first * LANES, LANES), LANES)]
+                two = rows_in[k, :, pl.ds(pl.multiple_of(after * LANES, LANES), LANES)]
+                both = jnp.where(lanes >= shift, one, two)
+                return pltpu.roll(both, lax.rem(LANES - shift, LANES), 1)
+
+            for t in range(5):
+                ends = [kk for kk in range(SIDE)
+                        if BLK * kk < LANES * (t + 1) and BLK * (kk + 1) > LANES * t]
+                value = window(t, ends[0])
+                if len(ends) > 1:
+                    edge = BLK * ends[1] - LANES * t
+                    value = jnp.where(lanes < edge, value, window(t, ends[1]))
+                hi, lo = split(value)
+                cols = slice(LANES * t, LANES * (t + 1))
+                stack[d, pl.ds(at_hi, BLK), cols] = hi
+                stack[d, pl.ds(at_lo, BLK), cols] = lo
+
+    store_rows(c)
 
     @pl.loop(1, OWN)
     def _(j):
@@ -270,15 +293,45 @@
         rcopy(vsend.at[4 * pa + pc], vin.at[sub, body], vs.at[peer], vr.at[sub], (owner, peer)).start()
 
     vin[sub, body] = vsend[4 * a + c]
-    store_rows(c, mat_ref[...])
+
+    @pl.loop(1, SUB)
+    def _(j):
+        peer = lax.rem(sub + j, SUB)
+        rcopy(offs.at[0], offs_in.at[peer], os.at[peer], orr.at[peer], (owner, peer)).wait_recv()
+
+    lane1 = iota((1, LANES), 1)
+    extra = jnp.where((lane1 & (HALF - 1)) >= SLOT, float(BLK), 0.0)
+    for m in range(SUB // 2):
+        one, two = offs_in[2 * m], offs_in[2 * m + 1]
+        for h in range(2):
+            if h == 0:
+                row = jnp.where(lane1 < HALF, one, half_swap(two)) + extra
+            else:
+                row = jnp.where(lane1 < HALF, half_swap(one), two) + extra
+            rowi = row.astype(jnp.int32)
+            cols = pl.ds(LANES * m, LANES)
+            land[h, :, cols] = (iota((PACK, LANES), 0) == rowi).astype(F32).astype(BF16)
+            down = jnp.broadcast_to(row, (LANES, LANES)).T.astype(jnp.int32)
+            for t, width in ((0, LANES), (1, LANES), (2, PACK - 2 * LANES)):
+                hit = (down == iota((LANES, LANES), 1) + LANES * t).astype(F32).astype(BF16)
+                land_t[h, cols, LANES * t:LANES * t + width] = hit[:, :width]
+
+    mat_copy(0, prevc, top, c_left).wait_recv()
+    mat_copy(4, prevc, top, c_right).start()
+    mat_copy(2, nextc, bottom, c_right).wait_recv()
+    mat_copy(5, nextc, bottom, c_left).start()
+
 
     for n, slot in ((0, prevc), (1, nextc), (2, oppc)):
-        rcopy(inv_ref, inv_in.at[slot], ivs.at[n], ivr.at[n], c_right).wait_recv()
+        inv_copy(n, slot, c_right).wait_recv()
     for k in range(4):
-        hi, lo = split(inv_in[k])
-        where_to = 2 * (k // 2) * BLK
-        mstack[k % 2, where_to:where_to + BLK, :] = hi
-        mstack[k % 2, where_to + BLK:where_to + 2 * BLK, :] = lo
+        inv_full[k, :, 0:LANES] = inv_in[k, 0:BLK]
+        for g in range(BLK // TAIL):
+            inv_full[k, TAIL * g:TAIL * (g + 1), LANES:BLK] = inv_in[
+                k, BLK:, 16 * g:16 * (g + 1)]
+        hi, lo = split(inv_full[k])
+        mstack[k, 0:BLK] = hi
+        mstack[k, BLK:] = lo
 
     @pl.loop(1, SUB)
     def _(j):
@@ -298,14 +351,29 @@
     values = side_by_side(vin[...].reshape(SUB * HALF, LANES))
     r = jnp.where(low_pack, fold(dot(land[0], values)), fold(dot(land[1], values)))
 
+    def spread(x):
+        keep = low_half(x.shape)
+        hi = x.astype(BF16).astype(F32)
+        rem = x - hi
+        mid = rem.astype(BF16).astype(F32)
+        lo = rem - mid
+        hi_, mid_, lo_ = half_swap(hi), half_swap(mid), half_swap(lo)
+        first = (jnp.where(keep, hi, mid_), jnp.where(keep, lo, lo_))
+        second = (jnp.where(keep, hi_, mid), jnp.where(keep, lo_, lo))
+        return tuple(jnp.concatenate(p, axis=1).astype(BF16) for p in (first, second))
+
+    def gathered(x):
+        return x[:, :LANES] + half_swap(x[:, :LANES]) + x[:, LANES:]
+
     def precond(v):
-        out = []
-        for kk in range(2):
-            got = dot(mstack[kk], side_by_side(v[kk * BLK:(kk + 1) * BLK]))
-            got = fold(got)
-            out.append(jnp.where(low_blk, got[:BLK] + got[BLK:2 * BLK],
-                                 got[2 * BLK:3 * BLK] + got[3 * BLK:]))
-        return jnp.concatenate(out, axis=0)
+        parts = spread(v)
+        done = []
+        for k in range(4):
+            lo_row = (k % 2) * BLK
+            got = dot(mstack[k], parts[k // 2][lo_row:lo_row + BLK])
+            done.append(gathered(got[:BLK] + got[BLK:]))
+        return jnp.concatenate(
+            [jnp.where(low_blk, done[kk], done[2 + kk]) for kk in range(2)], axis=0)
 
     nexta, preva, oppa = ring(a, 1), ring(a, -1), ring(a, 2)
     a_right, a_left, a_opp = (owner, at(nexta, c)), (owner, at(preva, c)), (owner, at(oppa, c))
@@ -315,14 +383,18 @@
         source = gin.at[it, slot, part] if forward else gsend.at[it, part]
         return rcopy(source, gin.at[it, slot, part], gs.at[it, n], gr.at[it, n], dev)
 
-    def widen(ra, x):
-        hi = x.astype(BF16).astype(F32)
-        lo = x - hi
-        first = jnp.where(low_pack, hi, half_swap(lo)).astype(BF16)
-        second = jnp.where(low_pack, half_swap(hi), lo).astype(BF16)
-        for k in range(4):
-            piece = (first if k < 2 else second)[(k % 2) * BLK:(k % 2 + 1) * BLK]
-            wide[pl.ds(pl.multiple_of(at(ra, k) * BLK, 16), BLK), :] = piece
+    def widen(d, x):
+        first, second = spread(x)
+        wide[d, 0:PACK] = first
+        wide[d, PACK:] = second
+
+    def product(d):
+        out = []
+        for h in range(2):
+            got = dot(stack[d, PACK * h:PACK * (h + 1), 0:2 * PACK], wide[d])
+            got = got + dot(stack[d, PACK * (2 + h):PACK * (3 + h), 0:2 * PACK], wide[d])
+            out.append(gathered(got))
+        return jnp.where(low_pack, out[0], out[1])
 
     def gather_start(it, v, sums):
         gsend[it, 0:PACK] = v
@@ -331,33 +403,29 @@
         vec_copy(it, 2, a, rest, a_left).start()
         vec_copy(it, 1, a, rest, a_right).start()
         vec_copy(it, 3, a, head, a_left).start()
-        widen(a, v)
+        widen(0, v)
 
     def gather_pass(it):
         vec_copy(it, 0, preva, head, a_left).wait_recv()
         vec_copy(it, 4, preva, head, a_right, True).start()
         vec_copy(it, 2, nexta, rest, a_right).wait_recv()
         vec_copy(it, 5, nexta, rest, a_left, True).start()
+
+    def gather_near(it):
         vec_copy(it, 1, preva, rest, a_left).wait_recv()
-        widen(preva, gin[it, preva, 0:PACK])
+        widen(3, gin[it, preva, 0:PACK])
         vec_copy(it, 3, nexta, head, a_right).wait_recv()
-        widen(nexta, gin[it, nexta, 0:PACK])
+        widen(1, gin[it, nexta, 0:PACK])
 
     def gather_end(it, sums):
         vec_copy(it, 4, oppa, head, a_right).wait_recv()
         vec_copy(it, 5, oppa, rest, a_left).wait_recv()
-        widen(oppa, gin[it, oppa, 0:PACK])
+        widen(2, gin[it, oppa, 0:PACK])
         total = sums
         for ra in (preva, nexta, oppa):
             total = total + gin[it, ra, PACK:VEC]
         return total
 
-    def product():
-        got = dot(stack[...], wide[...])
-        got = got[:SIDE * BLK] + got[SIDE * BLK:]
-        got = got + half_swap(got)
-        return jnp.where(low_pack, got[:PACK], got[PACK:])
-
     def column_sum(x, y):
         s = jnp.sum(x * y, axis=0, keepdims=True)
         return s + half_swap(s)
@@ -372,17 +440,18 @@
     nothing = jnp.zeros((8, LANES), F32)
     gather_start(0, u, nothing)
     gather_pass(0)
+    gather_near(0)
 
     mat_copy(1, prevc, bottom, c_left).wait_recv()
-    store_rows(prevc, rows_in[prevc])
+    store_rows(prevc)
     mat_copy(3, nextc, top, c_right).wait_recv()
-    store_rows(nextc, rows_in[nextc])
+    store_rows(nextc)
     mat_copy(4, oppc, top, c_right).wait_recv()
     mat_copy(5, oppc, bottom, c_left).wait_recv()
-    store_rows(oppc, rows_in[oppc])
+    store_rows(oppc)
 
     gather_end(0, nothing)
-    w = product()
+    w = product(0) + product(1) + product(2) + product(3)
 
     gamma = alpha = None
     x = p = s = q = z = None
@@ -390,9 +459,12 @@
         sums = partial_sums(r, u, w)
         m = precond(w)
         gather_start(it, m, sums)
+        partial[...] = product(0)
         gather_pass(it)
+        gather_near(it)
+        partial[...] = partial[...] + product(1) + product(3)
         total = gather_end(it, sums)
-        n = product()
+        n = partial[...] + product(2)
         gamma_new, delta = total[0:1], total[1:2]
         if it == 1:
             alpha = gamma_new / delta
@@ -492,7 +564,7 @@
             part = head if n_ in (0, 3, 4) else rest
             vec_copy(it, n_, a, part, a_right).wait_send()
     for n_ in range(3):
-        rcopy(inv_ref, inv_in.at[c], ivs.at[n_], ivr.at[n_], c_right).wait_send()
+        inv_copy(n_, c, c_right).wait_send()
         rcopy(ssend, sin.at[n_], ss.at[n_], sr.at[n_], a_right).wait_send()
         rcopy(rbuf.at[pl.ds(0, BLK)], rin.at[c], rs.at[n_], rr.at[n_], c_right).wait_send()
 
@@ -533,6 +605,11 @@
             corr_ref[:, where_to:where_to + LANES] = value
 
 
+def hand_on(corr_in, resid_in, corr_out, resid_out):
+    corr_out[...] = corr_in[...]
+    resid_out[...] = resid_in[...]
+
+
 def shards(residual, counts, assembly, level_two, block_inverse):
     vmem = pl.BlockSpec(memory_space=pltpu.VMEM)
     smem = pl.BlockSpec(memory_space=pltpu.SMEM)
@@ -540,19 +617,23 @@
     V = pltpu.VMEM
     dma = pltpu.SemaphoreType.DMA
     scratch = [
+        V(residual.shape, F32), V((PRIM, SIDE, SUB * BLK), jnp.int32), V((BLK, BLK), F32),
+        V((BLK + TAIL, LANES), F32),
         V((OWN, 8, LANES), F32), V((OWN, 1, LANES), F32),
         V((OWN, 8, LANES), F32), V((OWN, 1, LANES), F32),
         V((OWN, 8, LANES), F32), V((OWN, 1, LANES), F32),
         V((OWN, 8, LANES), F32), V((OWN, 1, LANES), F32),
         V((SIDE, 1, LANES), F32), V((SUB, 1, LANES), F32), V((8, 256), F32),
-        V((SIDE, BLK, SUB * BLK), F32), V((SIDE, BLK, BLK), F32),
-        V((2 * SIDE * BLK, SUB * BLK), BF16), V((2, SIDE * BLK, BLK), BF16),
+        V((SIDE, BLK, SUB * BLK), F32), V((SIDE, BLK + TAIL, LANES), F32),
+        V((SIDE, BLK, BLK), F32),
+        V((SIDE, 2 * SIDE * BLK, 5 * LANES), BF16), V((SIDE, 2 * BLK, BLK), BF16),
         V((SUB, MSG, LANES), F32), V((SUB, HALF, LANES), F32),
         V((2, PACK, SUB * HALF), BF16), V((2, SUB * HALF, PACK), BF16), V((4 * LANES, 256), BF16),
         V((ITERS, VEC, LANES), F32), V((ITERS, SIDE, VEC, LANES), F32),
-        V((SUB * BLK, LANES), BF16), V((8, LANES), F32), V((3, 8, LANES), F32),
+        V((SIDE, SIDE * BLK, 2 * LANES), BF16), V((8, LANES), F32), V((3, 8, LANES), F32),
         V((SUB, HALF, LANES), F32), V((SUB, MSG, LANES), F32), V((4 * LANES, 256), F32),
-        V((PACK, LANES), F32), V((SIDE, BLK, LANES), F32), V((256, 256), F32),
+        V((PACK, LANES), F32), V((SIDE, BLK, LANES), F32), V((256, 256), F32), V((PACK, LANES), F32),
+        dma((4,)),
         dma((OWN,)), dma((OWN,)), dma((OWN,)), dma((OWN,)),
         dma((OWN,)), dma((OWN,)), dma((OWN,)), dma((OWN,)),
         dma((SUB,)), dma((SUB,)), dma((6,)), dma((6,)), dma((3,)), dma((3,)),
@@ -565,13 +646,21 @@
             jax.ShapeDtypeStruct(residual.shape, F32),
             jax.ShapeDtypeStruct((BLK, 8 * OWN), F32),
         ),
-        in_specs=[vmem, smem, vmem, vmem, vmem],
+        in_specs=[smem, anywhere, anywhere, anywhere, anywhere],
         out_specs=(vmem, vmem),
         scratch_shapes=scratch,
         compiler_params=pltpu.CompilerParams(
-            collective_id=0, has_side_effects=True, vmem_limit_bytes=56 * 1024 * 1024
+            collective_id=0, has_side_effects=True, vmem_limit_bytes=44 * 1024 * 1024
         ),
-    )(residual, counts, assembly[0], level_two[0], block_inverse[0])
+    )(counts, residual, jnp.transpose(assembly[0], (1, 0, 2)), level_two[0], block_inverse[0])
+    corr, resid = pl.pallas_call(
+        hand_on,
+        out_shape=(
+            jax.ShapeDtypeStruct(corr.shape, F32), jax.ShapeDtypeStruct(resid.shape, F32)
+        ),
+        in_specs=[vmem, vmem],
+        out_specs=(vmem, vmem),
+    )(corr, resid)
     return corr, resid[None]
 
 

time: 127 us -> 113 us (0.89)
  Pallas kernels: 120 us -> 105 us
    pallas_call x1, Pallas kernels: 120 us -> 104 us  [shards(): pl.pallas_call(kernel, out_shape=(jax.ShapeDtypeStruct(residual.shape, F3...]
    pallas_call x0 -> x1, Pallas kernels: none -> 1.7 us  [shards(): pl.pallas_call(hand_on, out_shape=(jax.ShapeDtypeStruct(corr.shape, F32),...]
    unnamed x3 -> x14, local copies, waits for them, and re-layouts: 5.89 us -> 6.42 us
where the time goes in v2:
time: 113 us; the launch traced here: 112 us
  Pallas kernels  105 us (93%)
  local copies, waits for them, and re-layouts  6.42 us (6%)
    pallas_call x1, Pallas kernels, shards(): pl.pallas_call(kernel, out_shape=(jax.ShapeDtypeStruct(residual.shape, F3...  104 us
    unnamed x14, local copies, waits for them, and re-layouts  6.42 us

profile of v2, /device:TPU:1, one launch (start us, length us, event | category | flops | bytes accessed | tf_op | source)
XLA Modules:
  0.0 112.3 jit_solution(7956350715068039692)
XLA Ops:
  0.6 0.0 copy-start
  0.6 1.3 %copy-done = s32[1,4,36,2304]{3,1,2,0:T(4,128)S(1)} copy-done((s32[1,4,36,2304]{3,1,2,0:T(4,128)S(1)}, s32[1,4,36,2304]{3,1,2,0:T(4,128)}, u32[]{:S(2)}) %copy-start) | copy-done | bytes 1327128
  2.0 0.0 copy-start.1
  2.0 1.3 %copy-done.1 = f32[1,144,2304]{2,1,0:T(8,128)S(1)} copy-done((f32[1,144,2304]{2,1,0:T(8,128)S(1)}, f32[1,144,2304]{2,1,0:T(8,128)}, u32[]{:S(2)}) %copy-start.1) | copy-done | bytes 1327128
  3.3 0.0 copy-start.2
  3.3 0.9 copy-done.2
  4.2 0.0 copy-start.3
  4.2 0.9 copy-done.3
  5.1 0.0 copy-start.6
  5.1 0.7 copy-done.6
  5.8 103.5 %shard_map.68 = (f32[8,4608]{1,0:T(8,128)S(1)}, f32[144,256]{1,0:T(8,128)S(1)}) custom-call(s32[1,4]{1,0:T(1,128)S(1)} %copy-done.6, f32[8,4608]{1,0:T(8,128)S(1)} %copy-done.2, s32[36,4,2304]{2,1,0:T(4,128)S(1)} %bitcast.6, f32[144,2304]{1,0:T(8,128)S(1)} %bitcast.7, f32[144,144]{1,0:T(8,128)S(1)} %bitcast.8), custom_call_target="tpu_custom_call" | custom-call | tf_op jit(solution)/shard_map/pallas_call | solution.py:643
  109.3 0.0 copy-start.4
  109.3 0.6 copy-done.4
  109.9 0.0 copy-start.5
  110.0 0.7 copy-done.5
  110.6 1.7 %shard_map.69 = (f32[8,4608]{1,0:T(8,128)}, f32[144,256]{1,0:T(8,128)}) custom-call(f32[8,4608]{1,0:T(8,128)} %copy-done.4, f32[144,256]{1,0:T(8,128)} %copy-done.5), custom_call_target="tpu_custom_call" | custom-call | tf_op jit(solution)/shard_map/pallas_call | solution.py:656
Async XLA Ops:
  0.6 1.3 %copy-start = (s32[1,4,36,2304]{3,1,2,0:T(4,128)S(1)}, s32[1,4,36,2304]{3,1,2,0:T(4,128)}, u32[]{:S(2)}) copy-start(s32[1,4,36,2304]{3,1,2,0:T(4,128)} %param.7) | copy-start | bytes 3981316
  2.0 1.3 %copy-start.1 = (f32[1,144,2304]{2,1,0:T(8,128)S(1)}, f32[1,144,2304]{2,1,0:T(8,128)}, u32[]{:S(2)}) copy-start(f32[1,144,2304]{2,1,0:T(8,128)} %param.8) | copy-start | bytes 3981316
  3.3 0.9 copy-start.2
  4.2 0.9 copy-start.3
  5.1 0.7 copy-start.6
  109.3 0.7 copy-start.4
  109.9 0.7 copy-start.5

commit v3 on v2

--- a/solution.py
+++ b/solution.py
@@ -1,5 +1,3 @@
-import functools
-
 import jax
 import jax.numpy as jnp
 from jax import lax
@@ -22,7 +20,7 @@
 MSG = 40
 VEC = PACK + 8
 TAIL = 24
-CUT = 152
+CUTS = (0, 72, 224, VEC)
 
 
 def iota(shape, dim):
@@ -35,10 +33,6 @@
 
 def dot_nt(a, b):
     return lax.dot_general(a, b, (((1,), (1,)), ((), ())), preferred_element_type=F32)
-
-
-def dot_tn(a, b):
-    return lax.dot_general(a, b, (((0,), (0,)), ((), ())), preferred_element_type=F32)
 
 
 def split(x):
@@ -64,16 +58,16 @@
 
 
 def kernel(
-    cnt_ref, res_hbm, asm_hbm, mat_hbm, inv_hbm,
+    cnt_hbm, res_hbm, asm_hbm, mat_hbm, inv_hbm,
     corr_ref, resid_ref,
-    res_ref, asm_ref, inv_ref, inv_out,
+    cnt_ref, res_ref, asm_ref, inv_ref, inv_out,
     zmain, ztail, zmain_in, ztail_in,
     cmain, ctail, cmain_in, ctail_in,
     offs, offs_in, info,
     rows_in, inv_in, inv_full, stack, mstack,
-    vsend, vin, land, land_t, pick,
+    vsend, vin, land, land_t, pick, pick_t,
     gsend, gin, wide, ssend, sin,
-    psend, pin, back, rbuf, rin, local, partial,
+    psend, pin, back, rbuf, rin, local, partial, by_rows, answers,
     loads,
     zs_m, zr_m, zs_t, zr_t, cs_m, cr_m, cs_t, cr_t,
     os, orr, ms, mr, ivs, ivr, vs, vr, gs, gr, ss, sr, ps, pr, rs, rr,
@@ -99,21 +93,29 @@
 
     barrier = pltpu.get_barrier_semaphore()
 
-    @pl.loop(1, OWN)
-    def _(j):
-        pl.semaphore_signal(barrier, inc=1, device_id=(lax.rem(owner + j, OWN), sub),
-                            device_id_type=pl.DeviceIdType.MESH)
+    def each_owner(act):
+        act((owner + OWN // 2) & (OWN - 1))
+
+        @pl.loop(1, OWN // 2)
+        def _(i):
+            act((owner + (OWN // 2 + i)) & (OWN - 1))
+            act((owner + (OWN // 2 - i)) & (OWN - 1))
+
+    def greet(dev):
+        pl.semaphore_signal(barrier, inc=1, device_id=dev, device_id_type=pl.DeviceIdType.MESH)
+
+    each_owner(lambda peer: greet((peer, sub)))
 
     @pl.loop(1, SUB)
     def _(j):
-        pl.semaphore_signal(barrier, inc=1, device_id=(owner, lax.rem(sub + j, SUB)),
-                            device_id_type=pl.DeviceIdType.MESH)
+        greet((owner, (sub + j) & (SUB - 1)))
 
     fetches = [
         pltpu.make_async_copy(res_hbm, res_ref, loads.at[0]),
         pltpu.make_async_copy(asm_hbm, asm_ref, loads.at[1]),
         pltpu.make_async_copy(inv_hbm, inv_ref, loads.at[2]),
         pltpu.make_async_copy(mat_hbm, rows_in.at[c], loads.at[3]),
+        pltpu.make_async_copy(cnt_hbm, cnt_ref, loads.at[4]),
     ]
     for fetch in fetches:
         fetch.start()
@@ -150,6 +152,7 @@
         inv_out[BLK:, 16 * g:16 * (g + 1)] = inv_ref[TAIL * g:TAIL * (g + 1), LANES:BLK]
 
     fetches[1].wait()
+    fetches[4].wait()
     col = iota((8, SUB * BLK), 1)
     holder_of = col // BLK
     which = jnp.where(iota((8, SUB * BLK), 0) == 0, col - holder_of * BLK, holder_of)
@@ -185,15 +188,6 @@
 
     pl.semaphore_wait(barrier, OWN - 1 + SUB - 1)
 
-    @pl.loop(1, OWN)
-    def _(j):
-        peer = lax.rem(owner + j, OWN)
-        rcopy(zmain.at[peer], zmain_in.at[owner], zs_m.at[peer], zr_m.at[owner], (peer, sub)).start()
-        rcopy(ztail.at[peer], ztail_in.at[owner], zs_t.at[peer], zr_t.at[owner], (peer, sub)).start()
-
-    def off_copy(peer, pa):
-        return rcopy(offs.at[pa], offs_in.at[sub], os.at[peer], orr.at[sub], (owner, peer))
-
     def group_of(peer):
         px, py = peer // SIDE, lax.rem(peer, SIDE)
         return px * (1 - core) + py * core, py * (1 - core) + px * core
@@ -202,26 +196,37 @@
     def _(j):
         peer = lax.rem(sub + j, SUB)
         pa, _pc = group_of(peer)
-        off_copy(peer, pa).start()
-
-    nextc, prevc = ring(c, 1), ring(c, -1)
-    oppc = ring(c, 2)
+        rcopy(offs.at[pa], offs_in.at[sub], os, orr, (owner, peer)).start()
+
+    nextc, prevc, oppc = ring(c, 1), ring(c, -1), ring(c, 2)
     c_right, c_left, c_opp = (owner, at(a, nextc)), (owner, at(a, prevc)), (owner, at(a, oppc))
-    top, bottom = pl.ds(0, BLK // 2), pl.ds(BLK // 2, BLK // 2)
-
-    def mat_copy(n, slot, part, dev):
-        piece = rows_in.at[slot, part]
-        return rcopy(piece, piece, ms.at[n], mr.at[n], dev)
-
-    def inv_copy(n, slot, dev):
-        return rcopy(inv_out, inv_in.at[slot], ivs.at[n], ivr.at[n], dev)
-
-    mat_copy(0, c, top, c_right).start()
-    mat_copy(2, c, bottom, c_left).start()
-    mat_copy(1, c, bottom, c_right).start()
-    mat_copy(3, c, top, c_left).start()
-    for n, dev in ((0, c_right), (1, c_left), (2, c_opp)):
-        inv_copy(n, c, dev).start()
+    half = BLK // 2
+    top, bottom = pl.ds(0, half), pl.ds(half, half)
+    cuts = [top, bottom, bottom, top] + [
+        pl.ds(start + at_row, rows) for start in (0, half)
+        for at_row, rows in ((0, 40), (40, 32))]
+
+    def mat_copy(n, slot, dev):
+        piece = rows_in.at[slot, cuts[n]]
+        return rcopy(piece, piece, ms, mr.at[n], dev)
+
+    for dev in (c_opp, c_right, c_left):
+        rcopy(inv_out, inv_in.at[c], ivs, ivr, dev).start()
+    for n in range(2):
+        mat_copy(n, c, c_right).start()
+        mat_copy(2 + n, c, c_left).start()
+
+    def send_residual(peer):
+        rcopy(zmain.at[peer], zmain_in.at[owner], zs_m, zr_m, (peer, sub)).start()
+        rcopy(ztail.at[peer], ztail_in.at[owner], zs_t, zr_t, (peer, sub)).start()
+
+    each_owner(send_residual)
+
+    others, peers, three = pl.ds(0, OWN - 1), pl.ds(0, SUB - 1), pl.ds(0, SIDE - 1)
+    z_main = rcopy(zmain.at[others], zmain_in.at[others], zs_m, zr_m, c_right)
+    z_tail = rcopy(ztail.at[others], ztail_in.at[others], zs_t, zr_t, c_right)
+    all_offs = rcopy(offs_in.at[peers], offs_in.at[peers], os, orr, c_right)
+    all_inv = rcopy(inv_in.at[three], inv_in.at[three], ivs, ivr, c_right)
 
     zmain_in[owner] = zmain[owner]
     ztail_in[owner] = ztail[owner]
@@ -262,11 +267,8 @@
 
     store_rows(c)
 
-    @pl.loop(1, OWN)
-    def _(j):
-        peer = lax.rem(owner + j, OWN)
-        rcopy(zmain.at[peer], zmain_in.at[peer], zs_m.at[peer], zr_m.at[peer], (peer, sub)).wait_recv()
-        rcopy(ztail.at[peer], ztail_in.at[peer], zs_t.at[peer], zr_t.at[peer], (peer, sub)).wait_recv()
+    z_main.wait_recv()
+    z_tail.wait_recv()
 
     local[:, 0:LANES] = zmain_in[...].reshape(8 * OWN, LANES)
     for k in range(4):
@@ -286,18 +288,18 @@
             vsend[4 * ra + 2 * t + 1] = jnp.where(low_msg, half_swap(first), second)
     body = pl.ds(0, MSG)
 
-    @pl.loop(1, SUB)
-    def _(j):
-        peer = lax.rem(sub + j, SUB)
-        pa, pc = group_of(peer)
-        rcopy(vsend.at[4 * pa + pc], vin.at[sub, body], vs.at[peer], vr.at[sub], (owner, peer)).start()
+    far = sorted(((da, dc) for da in range(4) for dc in range(4) if da or dc),
+                 key=lambda d: -(min(d[0], 4 - d[0]) + min(d[1], 4 - d[1])))
+    for da, dc in far:
+        pa, pc = ring(a, da), ring(c, dc)
+        rcopy(vsend.at[4 * pa + pc], vin.at[sub, body], vs, vr, (owner, at(pa, pc))).start()
+    all_vals = rcopy(vin.at[peers, body], vin.at[peers, body], vs, vr, c_right)
 
     vin[sub, body] = vsend[4 * a + c]
 
-    @pl.loop(1, SUB)
-    def _(j):
-        peer = lax.rem(sub + j, SUB)
-        rcopy(offs.at[0], offs_in.at[peer], os.at[peer], orr.at[peer], (owner, peer)).wait_recv()
+    all_offs.wait_recv()
+
+    pick_t[...] = pick[...].astype(F32).T.astype(BF16)
 
     lane1 = iota((1, LANES), 1)
     extra = jnp.where((lane1 & (HALF - 1)) >= SLOT, float(BLK), 0.0)
@@ -316,14 +318,13 @@
                 hit = (down == iota((LANES, LANES), 1) + LANES * t).astype(F32).astype(BF16)
                 land_t[h, cols, LANES * t:LANES * t + width] = hit[:, :width]
 
-    mat_copy(0, prevc, top, c_left).wait_recv()
-    mat_copy(4, prevc, top, c_right).start()
-    mat_copy(2, nextc, bottom, c_right).wait_recv()
-    mat_copy(5, nextc, bottom, c_left).start()
-
-
-    for n, slot in ((0, prevc), (1, nextc), (2, oppc)):
-        inv_copy(n, slot, c_right).wait_recv()
+    mat_copy(0, prevc, c_left).wait_recv()
+    mat_copy(4, prevc, c_right).start()
+    mat_copy(2, nextc, c_right).wait_recv()
+    mat_copy(6, nextc, c_left).start()
+
+
+    all_inv.wait_recv()
     for k in range(4):
         inv_full[k, :, 0:LANES] = inv_in[k, 0:BLK]
         for g in range(BLK // TAIL):
@@ -333,10 +334,12 @@
         mstack[k, 0:BLK] = hi
         mstack[k, BLK:] = lo
 
-    @pl.loop(1, SUB)
-    def _(j):
-        peer = lax.rem(sub + j, SUB)
-        rcopy(vsend.at[0], vin.at[peer, body], vs.at[peer], vr.at[peer], (owner, peer)).wait_recv()
+    mat_copy(1, prevc, c_left).wait_recv()
+    store_rows(prevc)
+    mat_copy(3, nextc, c_right).wait_recv()
+    store_rows(nextc)
+
+    all_vals.wait_recv()
 
     low_pack = low_half((PACK, LANES))
     low_blk = low_half((BLK, LANES))
@@ -357,13 +360,14 @@
         rem = x - hi
         mid = rem.astype(BF16).astype(F32)
         lo = rem - mid
-        hi_, mid_, lo_ = half_swap(hi), half_swap(mid), half_swap(lo)
-        first = (jnp.where(keep, hi, mid_), jnp.where(keep, lo, lo_))
-        second = (jnp.where(keep, hi_, mid), jnp.where(keep, lo_, lo))
+        mid_ = half_swap(mid)
+        first = (jnp.where(keep, hi, mid_), jnp.where(keep, lo, 0.0))
+        second = (jnp.where(keep, mid_, hi), jnp.where(keep, 0.0, lo))
         return tuple(jnp.concatenate(p, axis=1).astype(BF16) for p in (first, second))
 
     def gathered(x):
-        return x[:, :LANES] + half_swap(x[:, :LANES]) + x[:, LANES:]
+        one = x[:, :LANES] + x[:, LANES:]
+        return one + half_swap(one)
 
     def precond(v):
         parts = spread(v)
@@ -377,11 +381,14 @@
 
     nexta, preva, oppa = ring(a, 1), ring(a, -1), ring(a, 2)
     a_right, a_left, a_opp = (owner, at(nexta, c)), (owner, at(preva, c)), (owner, at(oppa, c))
-    head, rest = pl.ds(0, CUT), pl.ds(CUT, VEC - CUT)
-
-    def vec_copy(it, n, slot, part, dev, forward=False):
-        source = gin.at[it, slot, part] if forward else gsend.at[it, part]
-        return rcopy(source, gin.at[it, slot, part], gs.at[it, n], gr.at[it, n], dev)
+    head, middle, tail = (pl.ds(CUTS[i], CUTS[i + 1] - CUTS[i]) for i in range(3))
+    parts = [head, pl.ds(CUTS[1], VEC - CUTS[1]), tail, pl.ds(0, CUTS[2]), middle, head, tail]
+    toward = [a_right, a_right, a_left, a_left, a_opp, a_right, a_left]
+
+    def vec_copy(it, n, slot):
+        part = parts[n]
+        source = gin.at[it, slot, part] if n > 4 else gsend.at[it, part]
+        return rcopy(source, gin.at[it, slot, part], gs.at[it], gr.at[it % 2, n], toward[n])
 
     def widen(d, x):
         first, second = spread(x)
@@ -396,30 +403,38 @@
             out.append(gathered(got))
         return jnp.where(low_pack, out[0], out[1])
 
+    def product_rows(k, chunks):
+        got = None
+        for d in chunks:
+            for first in (k, SIDE + k):
+                rows = stack[d, pl.ds(pl.multiple_of(first * BLK, 16), BLK), 0:2 * PACK]
+                term = dot(rows, wide[d])
+                got = term if got is None else got + term
+        got = gathered(got)
+        by_rows[k] = got if chunks[0] == 0 else by_rows[k] + got
+
     def gather_start(it, v, sums):
         gsend[it, 0:PACK] = v
         gsend[it, PACK:VEC] = sums
-        vec_copy(it, 0, a, head, a_right).start()
-        vec_copy(it, 2, a, rest, a_left).start()
-        vec_copy(it, 1, a, rest, a_right).start()
-        vec_copy(it, 3, a, head, a_left).start()
+        for n in (0, 2, 1, 3, 4):
+            vec_copy(it, n, a).start()
         widen(0, v)
 
     def gather_pass(it):
-        vec_copy(it, 0, preva, head, a_left).wait_recv()
-        vec_copy(it, 4, preva, head, a_right, True).start()
-        vec_copy(it, 2, nexta, rest, a_right).wait_recv()
-        vec_copy(it, 5, nexta, rest, a_left, True).start()
+        vec_copy(it, 0, preva).wait_recv()
+        vec_copy(it, 5, preva).start()
+        vec_copy(it, 2, nexta).wait_recv()
+        vec_copy(it, 6, nexta).start()
 
     def gather_near(it):
-        vec_copy(it, 1, preva, rest, a_left).wait_recv()
+        vec_copy(it, 1, preva).wait_recv()
         widen(3, gin[it, preva, 0:PACK])
-        vec_copy(it, 3, nexta, head, a_right).wait_recv()
+        vec_copy(it, 3, nexta).wait_recv()
         widen(1, gin[it, nexta, 0:PACK])
 
     def gather_end(it, sums):
-        vec_copy(it, 4, oppa, head, a_right).wait_recv()
-        vec_copy(it, 5, oppa, rest, a_left).wait_recv()
+        for n in (4, 5, 6):
+            vec_copy(it, n, oppa).wait_recv()
         widen(2, gin[it, oppa, 0:PACK])
         total = sums
         for ra in (preva, nexta, oppa):
@@ -439,19 +454,23 @@
     u = precond(r)
     nothing = jnp.zeros((8, LANES), F32)
     gather_start(0, u, nothing)
+    mat_copy(5, prevc, c_right).start()
+    mat_copy(7, nextc, c_left).start()
+    for k in (c, prevc, nextc):
+        product_rows(k, (0,))
     gather_pass(0)
     gather_near(0)
-
-    mat_copy(1, prevc, bottom, c_left).wait_recv()
-    store_rows(prevc)
-    mat_copy(3, nextc, top, c_right).wait_recv()
-    store_rows(nextc)
-    mat_copy(4, oppc, top, c_right).wait_recv()
-    mat_copy(5, oppc, bottom, c_left).wait_recv()
+    for k in (c, prevc, nextc):
+        product_rows(k, (1, 3))
+    gather_end(0, nothing)
+    for k in (c, prevc, nextc):
+        product_rows(k, (2,))
+    for n in range(4, 8):
+        mat_copy(n, oppc, c_right).wait_recv()
     store_rows(oppc)
-
-    gather_end(0, nothing)
-    w = product(0) + product(1) + product(2) + product(3)
+    product_rows(oppc, (0, 1, 3, 2))
+    w = jnp.concatenate(
+        [jnp.where(low_blk, by_rows[kk], by_rows[2 + kk]) for kk in range(2)], axis=0)
 
     gamma = alpha = None
     x = p = s = q = z = None
@@ -482,44 +501,42 @@
 
     sums = partial_sums(r, u, w)
     ssend[...] = sums
-    for n_, dev in ((0, a_right), (1, a_left), (2, a_opp)):
-        rcopy(ssend, sin.at[n_], ss.at[n_], sr.at[n_], dev).start()
-    total = sums
-    for n_ in range(3):
-        rcopy(ssend, sin.at[n_], ss.at[n_], sr.at[n_], a_right).wait_recv()
-        total = total + sin[n_]
+    for n, dev in ((2, a_opp), (0, a_right), (1, a_left)):
+        rcopy(ssend, sin.at[n], ss, sr, dev).start()
+    all_sums = rcopy(sin, sin, ss, sr, a_right)
+
+    low_slots = low_half((SUB * HALF, LANES))
+
+    def reply_of(v):
+        vs_ = side_by_side(v)
+        return jnp.where(low_slots, fold(dot(land_t[0], vs_)), fold(dot(land_t[1], vs_)))
+
+    for n, v in ((0, x), (1, u), (2, p)):
+        answers[n] = reply_of(v)
+    all_sums.wait_recv()
+    total = sums + sin[0] + sin[1] + sin[2]
     gamma_new, delta = total[0:1], total[1:2]
     beta = gamma_new / gamma
     alpha = gamma_new / (delta - beta * gamma_new / alpha)
-    s, p = w + beta * s, u + beta * p
-    x = x + alpha * p
-    r = r - alpha * s
-
-    xs = side_by_side(x)
-    low_slots = low_half((SUB * HALF, LANES))
-    reply = jnp.where(low_slots, fold(dot(land_t[0], xs)), fold(dot(land_t[1], xs)))
+    reply = answers[0] + alpha * (answers[1] + beta * answers[2])
     psend[...] = reply.reshape(SUB, HALF, LANES)
     mine = 4 * a + c
 
-    @pl.loop(1, SUB)
-    def _(j):
-        peer = lax.rem(sub + j, SUB)
-        rcopy(psend.at[peer, body], pin.at[mine], ps.at[peer], pr.at[mine], (owner, peer)).start()
+    for da, dc in far:
+        peer = at(ring(a, da), ring(c, dc))
+        rcopy(psend.at[peer, body], pin.at[mine], ps, pr, (owner, peer)).start()
+    all_back = rcopy(pin.at[peers], pin.at[peers], ps, pr, c_right)
 
     pin[mine] = psend[sub, body]
 
-    rbuf[...] = r
-    for n_, slot, dev in ((0, nextc, c_right), (1, prevc, c_left), (2, oppc, c_opp)):
+    rbuf[...] = r - alpha * (w + beta * s)
+    for slot, dev in ((oppc, c_opp), (nextc, c_right), (prevc, c_left)):
         source = rbuf.at[pl.ds(pl.multiple_of(lax.rem(slot, 2) * BLK, 8), BLK)]
-        rcopy(source, rin.at[c], rs.at[n_], rr.at[n_], dev).start()
+        rcopy(source, rin.at[c], rs, rr, dev).start()
+    all_resid = rcopy(rin.at[three], rin.at[three], rs, rr, c_right)
     rin[c] = rbuf[pl.ds(pl.multiple_of(lax.rem(c, 2) * BLK, 8), BLK)]
 
-    @pl.loop(1, SUB)
-    def _(j):
-        peer = lax.rem(sub + j, SUB)
-        pa, pc = group_of(peer)
-        slot = 4 * pa + pc
-        rcopy(psend.at[peer, body], pin.at[slot], ps.at[peer], pr.at[slot], (owner, peer)).wait_recv()
+    all_back.wait_recv()
 
     for ra in range(4):
         for t in range(2):
@@ -529,7 +546,7 @@
             back[LANES * ra + HALF:LANES * ra + HALF + MSG, cols] = jnp.where(
                 low_msg, half_swap(one), two)
     back_hi, back_lo = split(back[...])
-    mine_back = dot_tn(back_hi, pick[...]) + dot_tn(back_lo, pick[...])
+    mine_back = (dot(pick_t[...], back_hi) + dot(pick_t[...], back_lo)).T
     cmain[...] = mine_back[:, :LANES].reshape(OWN, 8, LANES)
     for k in range(4):
         tails = None
@@ -541,53 +558,34 @@
         for j in range(8):
             ctail[8 * k + j] = moved[j:j + 1, :]
 
-    @pl.loop(1, OWN)
-    def _(j):
-        peer = lax.rem(owner + j, OWN)
-        rcopy(cmain.at[peer], cmain_in.at[owner], cs_m.at[peer], cr_m.at[owner], (peer, sub)).start()
-        rcopy(ctail.at[peer], ctail_in.at[owner], cs_t.at[peer], cr_t.at[owner], (peer, sub)).start()
+    def send_correction(peer):
+        rcopy(cmain.at[peer], cmain_in.at[owner], cs_m, cr_m, (peer, sub)).start()
+        rcopy(ctail.at[peer], ctail_in.at[owner], cs_t, cr_t, (peer, sub)).start()
+
+    each_owner(send_correction)
+
+    c_main = rcopy(cmain.at[others], cmain_in.at[others], cs_m, cr_m, c_right)
+    c_tail = rcopy(ctail.at[others], ctail_in.at[others], cs_t, cr_t, c_right)
 
     cmain_in[owner] = cmain[owner]
     ctail_in[owner] = ctail[owner]
 
-    for n_, slot in ((0, prevc), (1, nextc), (2, oppc)):
-        rcopy(rbuf.at[pl.ds(0, BLK)], rin.at[slot], rs.at[n_], rr.at[n_], c_right).wait_recv()
+    all_resid.wait_recv()
     for t in range(2):
         one, two = rin[2 * t], rin[2 * t + 1]
         upper_half = jnp.where(low_blk, half_swap(one), two)
         lower_half = jnp.where(low_blk, one, half_swap(two))
         resid_ref[:, LANES * t:LANES * (t + 1)] = jnp.where(c < 2, lower_half, upper_half)
 
-    for n_ in range(6):
-        mat_copy(n_, c, top, c_right).wait_send()
-        for it in range(ITERS):
-            part = head if n_ in (0, 3, 4) else rest
-            vec_copy(it, n_, a, part, a_right).wait_send()
-    for n_ in range(3):
-        inv_copy(n_, c, c_right).wait_send()
-        rcopy(ssend, sin.at[n_], ss.at[n_], sr.at[n_], a_right).wait_send()
-        rcopy(rbuf.at[pl.ds(0, BLK)], rin.at[c], rs.at[n_], rr.at[n_], c_right).wait_send()
-
-    @pl.loop(1, SUB)
-    def _(j):
-        peer = lax.rem(sub + j, SUB)
-        rcopy(offs.at[0], offs_in.at[peer], os.at[peer], orr.at[peer], (owner, peer)).wait_send()
-        rcopy(vsend.at[0], vin.at[peer, body], vs.at[peer], vr.at[peer], (owner, peer)).wait_send()
-        rcopy(psend.at[peer, body], pin.at[peer], ps.at[peer], pr.at[peer], (owner, peer)).wait_send()
-
-    @pl.loop(1, OWN)
-    def _(j):
-        peer = lax.rem(owner + j, OWN)
-        rcopy(zmain.at[peer], zmain_in.at[peer], zs_m.at[peer], zr_m.at[peer], (peer, sub)).wait_send()
-        rcopy(ztail.at[peer], ztail_in.at[peer], zs_t.at[peer], zr_t.at[peer], (peer, sub)).wait_send()
-        rcopy(cmain.at[peer], cmain_in.at[peer], cs_m.at[peer], cr_m.at[peer], (peer, sub)).wait_recv()
-        rcopy(ctail.at[peer], ctail_in.at[peer], cs_t.at[peer], cr_t.at[peer], (peer, sub)).wait_recv()
-
-    @pl.loop(1, OWN)
-    def _(j):
-        peer = lax.rem(owner + j, OWN)
-        rcopy(cmain.at[peer], cmain_in.at[peer], cs_m.at[peer], cr_m.at[peer], (peer, sub)).wait_send()
-        rcopy(ctail.at[peer], ctail_in.at[peer], cs_t.at[peer], cr_t.at[peer], (peer, sub)).wait_send()
+    rcopy(rows_in.at[three], rows_in.at[three], ms, mr.at[0], c_right).wait_send()
+    for it in range(ITERS):
+        rcopy(gin.at[it, three], gin.at[it, three], gs.at[it], gr.at[0, 0], c_right).wait_send()
+    for sent in (z_main, z_tail, all_offs, all_inv, all_vals, all_sums, all_back, all_resid):
+        sent.wait_send()
+    c_main.wait_recv()
+    c_tail.wait_recv()
+    c_main.wait_send()
+    c_tail.wait_send()
 
     for k in range(4):
         tails = block_transpose(ctail_in[8 * k:8 * (k + 1)].reshape(8, LANES))
@@ -612,11 +610,11 @@
 
 def shards(residual, counts, assembly, level_two, block_inverse):
     vmem = pl.BlockSpec(memory_space=pltpu.VMEM)
-    smem = pl.BlockSpec(memory_space=pltpu.SMEM)
     anywhere = pl.BlockSpec(memory_space=pl.ANY)
     V = pltpu.VMEM
     dma = pltpu.SemaphoreType.DMA
     scratch = [
+        pltpu.SMEM(counts.shape, jnp.int32),
         V(residual.shape, F32), V((PRIM, SIDE, SUB * BLK), jnp.int32), V((BLK, BLK), F32),
         V((BLK + TAIL, LANES), F32),
         V((OWN, 8, LANES), F32), V((OWN, 1, LANES), F32),
@@ -629,16 +627,17 @@
         V((SIDE, 2 * SIDE * BLK, 5 * LANES), BF16), V((SIDE, 2 * BLK, BLK), BF16),
         V((SUB, MSG, LANES), F32), V((SUB, HALF, LANES), F32),
         V((2, PACK, SUB * HALF), BF16), V((2, SUB * HALF, PACK), BF16), V((4 * LANES, 256), BF16),
+        V((256, 4 * LANES), BF16),
         V((ITERS, VEC, LANES), F32), V((ITERS, SIDE, VEC, LANES), F32),
         V((SIDE, SIDE * BLK, 2 * LANES), BF16), V((8, LANES), F32), V((3, 8, LANES), F32),
         V((SUB, HALF, LANES), F32), V((SUB, MSG, LANES), F32), V((4 * LANES, 256), F32),
         V((PACK, LANES), F32), V((SIDE, BLK, LANES), F32), V((256, 256), F32), V((PACK, LANES), F32),
-        dma((4,)),
-        dma((OWN,)), dma((OWN,)), dma((OWN,)), dma((OWN,)),
-        dma((OWN,)), dma((OWN,)), dma((OWN,)), dma((OWN,)),
-        dma((SUB,)), dma((SUB,)), dma((6,)), dma((6,)), dma((3,)), dma((3,)),
-        dma((SUB,)), dma((SUB,)), dma((ITERS, 6)), dma((ITERS, 6)), dma((3,)), dma((3,)),
-        dma((SUB,)), dma((SUB,)), dma((3,)), dma((3,)),
+        V((SIDE, BLK, LANES), F32), V((3, SUB * HALF, LANES), F32),
+        dma((5,)),
+        dma, dma, dma, dma, dma, dma, dma, dma,
+        dma, dma, dma, dma((8,)), dma, dma,
+        dma, dma, dma((ITERS,)), dma((2, 7)), dma, dma,
+        dma, dma, dma, dma,
     ]
     corr, resid = pl.pallas_call(
         kernel,
@@ -646,11 +645,11 @@
             jax.ShapeDtypeStruct(residual.shape, F32),
             jax.ShapeDtypeStruct((BLK, 8 * OWN), F32),
         ),
-        in_specs=[smem, anywhere, anywhere, anywhere, anywhere],
+        in_specs=[anywhere] * 5,
         out_specs=(vmem, vmem),
         scratch_shapes=scratch,
         compiler_params=pltpu.CompilerParams(
-            collective_id=0, has_side_effects=True, vmem_limit_bytes=44 * 1024 * 1024
+            collective_id=0, has_side_effects=True, vmem_limit_bytes=62 * 1024 * 1024
         ),
     )(counts, residual, jnp.transpose(assembly[0], (1, 0, 2)), level_two[0], block_inverse[0])
     corr, resid = pl.pallas_call(

time: 113 us -> 98.3 us (0.87)
  Pallas kernels: 105 us -> 97.4 us
  local copies, waits for them, and re-layouts: 6.42 us -> 0 us
    pallas_call x1, Pallas kernels: 104 us -> 95.7 us  [shards(): pl.pallas_call(kernel, out_shape=(jax.ShapeDtypeStruct(residual.shape, F3...]
    unnamed x14 -> x0, local copies, waits for them, and re-layouts: 6.42 us -> none
where the time goes in v3:
time: 98.3 us; the launch traced here: 98.1 us
  Pallas kernels  97.4 us (99%)
    pallas_call x1, Pallas kernels, shards(): pl.pallas_call(kernel, out_shape=(jax.ShapeDtypeStruct(residual.shape, F3...  95.7 us

profile of v3, /device:TPU:1, one launch (start us, length us, event | category | flops | bytes accessed | tf_op | source)
XLA Modules:
  0.0 98.1 jit_solution(15561815966816985054)
XLA Ops:
  0.6 95.7 %shard_map.68 = (f32[8,4608]{1,0:T(8,128)}, f32[144,256]{1,0:T(8,128)}) custom-call(s32[1,4]{1,0:T(1,128)} %cnt_hbm.1, f32[8,4608]{1,0:T(8,128)} %res_hbm.1, s32[36,4,2304]{2,1,0:T(4,128)} %bitcast.6, f32[144,2304]{1,0:T(8,128)} %bitcast.7, f32[144,144]{1,0:T(8,128)} %bitcast.8), custom_call_target="tpu_custom_call" | custom-call | tf_op jit(solution)/shard_map/pallas_call | solution.py:642
  96.4 1.7 %shard_map.69 = (f32[8,4608]{1,0:T(8,128)}, f32[144,256]{1,0:T(8,128)}) custom-call(f32[8,4608]{1,0:T(8,128)} %get-tuple-element.6.corr_in, f32[144,256]{1,0:T(8,128)} %get-tuple-element.7.resid_in), custom_call_target="tpu_custom_call" | custom-call | tf_op jit(solution)/shard_map/pallas_call | solution.py:655

commit v4 on v3

--- a/solution.py
+++ b/solution.py
@@ -20,7 +20,7 @@
 MSG = 40
 VEC = PACK + 8
 TAIL = 24
-CUTS = (0, 72, 224, VEC)
+CUTS = (0, 72, 144, VEC)
 
 
 def iota(shape, dim):
@@ -202,9 +202,10 @@
     c_right, c_left, c_opp = (owner, at(a, nextc)), (owner, at(a, prevc)), (owner, at(a, oppc))
     half = BLK // 2
     top, bottom = pl.ds(0, half), pl.ds(half, half)
-    cuts = [top, bottom, bottom, top] + [
+    early, late = pl.ds(half, 40), pl.ds(half + 40, 32)
+    cuts = [top, early, bottom, pl.ds(0, 40)] + [
         pl.ds(start + at_row, rows) for start in (0, half)
-        for at_row, rows in ((0, 40), (40, 32))]
+        for at_row, rows in ((0, 40), (40, 32))] + [late, pl.ds(40, 32)]
 
     def mat_copy(n, slot, dev):
         piece = rows_in.at[slot, cuts[n]]
@@ -293,6 +294,8 @@
     for da, dc in far:
         pa, pc = ring(a, da), ring(c, dc)
         rcopy(vsend.at[4 * pa + pc], vin.at[sub, body], vs, vr, (owner, at(pa, pc))).start()
+    mat_copy(8, c, c_right).start()
+    mat_copy(9, c, c_left).start()
     all_vals = rcopy(vin.at[peers, body], vin.at[peers, body], vs, vr, c_right)
 
     vin[sub, body] = vsend[4 * a + c]
@@ -334,11 +337,6 @@
         mstack[k, 0:BLK] = hi
         mstack[k, BLK:] = lo
 
-    mat_copy(1, prevc, c_left).wait_recv()
-    store_rows(prevc)
-    mat_copy(3, nextc, c_right).wait_recv()
-    store_rows(nextc)
-
     all_vals.wait_recv()
 
     low_pack = low_half((PACK, LANES))
@@ -369,25 +367,22 @@
         one = x[:, :LANES] + x[:, LANES:]
         return one + half_swap(one)
 
-    def precond(v):
-        parts = spread(v)
+    def precond_half(parts, kk):
         done = []
-        for k in range(4):
-            lo_row = (k % 2) * BLK
-            got = dot(mstack[k], parts[k // 2][lo_row:lo_row + BLK])
+        for k in (kk, 2 + kk):
+            got = dot(mstack[k], parts[k // 2][kk * BLK:(kk + 1) * BLK])
             done.append(gathered(got[:BLK] + got[BLK:]))
-        return jnp.concatenate(
-            [jnp.where(low_blk, done[kk], done[2 + kk]) for kk in range(2)], axis=0)
+        return jnp.where(low_blk, done[0], done[1])
 
     nexta, preva, oppa = ring(a, 1), ring(a, -1), ring(a, 2)
     a_right, a_left, a_opp = (owner, at(nexta, c)), (owner, at(preva, c)), (owner, at(oppa, c))
-    head, middle, tail = (pl.ds(CUTS[i], CUTS[i + 1] - CUTS[i]) for i in range(3))
-    parts = [head, pl.ds(CUTS[1], VEC - CUTS[1]), tail, pl.ds(0, CUTS[2]), middle, head, tail]
-    toward = [a_right, a_right, a_left, a_left, a_opp, a_right, a_left]
+    head, tail, after = (pl.ds(CUTS[i], CUTS[i + 1] - CUTS[i]) for i in range(3))
+    parts_of = [head, pl.ds(CUTS[1], VEC - CUTS[1]), tail, head, after, head, tail, after]
+    toward = [a_right, a_right, a_left, a_left, a_opp, a_right, a_left, a_left]
 
     def vec_copy(it, n, slot):
-        part = parts[n]
-        source = gin.at[it, slot, part] if n > 4 else gsend.at[it, part]
+        part = parts_of[n]
+        source = gin.at[it, slot, part] if n in (5, 6) else gsend.at[it, part]
         return rcopy(source, gin.at[it, slot, part], gs.at[it], gr.at[it % 2, n], toward[n])
 
     def widen(d, x):
@@ -413,12 +408,21 @@
         got = gathered(got)
         by_rows[k] = got if chunks[0] == 0 else by_rows[k] + got
 
-    def gather_start(it, v, sums):
-        gsend[it, 0:PACK] = v
+    def gather_start(it, v, sums_of):
+        parts = spread(v)
+        first = precond_half(parts, 0)
+        gsend[it, 0:BLK] = first
+        for n in (0, 2):
+            vec_copy(it, n, a).start()
+        sums = sums_of()
+        second = precond_half(parts, 1)
+        gsend[it, BLK:PACK] = second
         gsend[it, PACK:VEC] = sums
-        for n in (0, 2, 1, 3, 4):
+        for n in (1, 3, 7, 4):
             vec_copy(it, n, a).start()
-        widen(0, v)
+        out = jnp.concatenate([first, second], axis=0)
+        widen(0, out)
+        return out, sums
 
     def gather_pass(it):
         vec_copy(it, 0, preva).wait_recv()
@@ -430,6 +434,7 @@
         vec_copy(it, 1, preva).wait_recv()
         widen(3, gin[it, preva, 0:PACK])
         vec_copy(it, 3, nexta).wait_recv()
+        vec_copy(it, 7, nexta).wait_recv()
         widen(1, gin[it, nexta, 0:PACK])
 
     def gather_end(it, sums):
@@ -451,14 +456,20 @@
         one, two = column_sum(r, u), column_sum(w, u)
         return jnp.where(row8 == 0, one, jnp.where(row8 == 1, two, 0.0))
 
-    u = precond(r)
     nothing = jnp.zeros((8, LANES), F32)
-    gather_start(0, u, nothing)
+    u, _ = gather_start(0, r, lambda: nothing)
     mat_copy(5, prevc, c_right).start()
     mat_copy(7, nextc, c_left).start()
+    mat_copy(1, prevc, c_left).wait_recv()
+    mat_copy(8, prevc, c_left).wait_recv()
+    store_rows(prevc)
+    mat_copy(3, nextc, c_right).wait_recv()
+    mat_copy(9, nextc, c_right).wait_recv()
+    store_rows(nextc)
+
+    gather_pass(0)
     for k in (c, prevc, nextc):
         product_rows(k, (0,))
-    gather_pass(0)
     gather_near(0)
     for k in (c, prevc, nextc):
         product_rows(k, (1, 3))
@@ -475,9 +486,7 @@
     gamma = alpha = None
     x = p = s = q = z = None
     for it in range(1, ITERS):
-        sums = partial_sums(r, u, w)
-        m = precond(w)
-        gather_start(it, m, sums)
+        m, sums = gather_start(it, w, lambda: partial_sums(r, u, w))
         partial[...] = product(0)
         gather_pass(it)
         gather_near(it)
@@ -635,8 +644,8 @@
         V((SIDE, BLK, LANES), F32), V((3, SUB * HALF, LANES), F32),
         dma((5,)),
         dma, dma, dma, dma, dma, dma, dma, dma,
-        dma, dma, dma, dma((8,)), dma, dma,
-        dma, dma, dma((ITERS,)), dma((2, 7)), dma, dma,
+        dma, dma, dma, dma((10,)), dma, dma,
+        dma, dma, dma((ITERS,)), dma((2, 8)), dma, dma,
         dma, dma, dma, dma,
     ]
     corr, resid = pl.pallas_call(

time: 98.3 us -> 97.5 us (level)
  no operation moved by 1% of the time
where the time goes in v4:
time: 97.5 us; the launch traced here: 97.3 us
  Pallas kernels  96.7 us (99%)
    pallas_call x1, Pallas kernels, shards(): pl.pallas_call(kernel, out_shape=(jax.ShapeDtypeStruct(residual.shape, F3...  95 us

profile of v4, /device:TPU:1, one launch (start us, length us, event | category | flops | bytes accessed | tf_op | source)
XLA Modules:
  0.0 97.3 jit_solution(14167250218540857751)
XLA Ops:
  0.6 95.0 %shard_map.68 = (f32[8,4608]{1,0:T(8,128)}, f32[144,256]{1,0:T(8,128)}) custom-call(s32[1,4]{1,0:T(1,128)} %cnt_hbm.1, f32[8,4608]{1,0:T(8,128)} %res_hbm.1, s32[36,4,2304]{2,1,0:T(4,128)} %bitcast.6, f32[144,2304]{1,0:T(8,128)} %bitcast.7, f32[144,144]{1,0:T(8,128)} %bitcast.8), custom_call_target="tpu_custom_call" | custom-call | tf_op jit(solution)/shard_map/pallas_call | solution.py:651
  95.6 1.7 %shard_map.69 = (f32[8,4608]{1,0:T(8,128)}, f32[144,256]{1,0:T(8,128)}) custom-call(f32[8,4608]{1,0:T(8,128)} %get-tuple-element.6.corr_in, f32[144,256]{1,0:T(8,128)} %get-tuple-element.7.resid_in), custom_call_target="tpu_custom_call" | custom-call | tf_op jit(solution)/shard_map/pallas_call | solution.py:664

commit v5 on v4

--- a/solution.py
+++ b/solution.py
@@ -211,11 +211,12 @@
         piece = rows_in.at[slot, cuts[n]]
         return rcopy(piece, piece, ms, mr.at[n], dev)
 
+    mat_copy(0, c, c_right).start()
+    mat_copy(2, c, c_left).start()
     for dev in (c_opp, c_right, c_left):
         rcopy(inv_out, inv_in.at[c], ivs, ivr, dev).start()
-    for n in range(2):
-        mat_copy(n, c, c_right).start()
-        mat_copy(2 + n, c, c_left).start()
+    mat_copy(1, c, c_right).start()
+    mat_copy(3, c, c_left).start()
 
     def send_residual(peer):
         rcopy(zmain.at[peer], zmain_in.at[owner], zs_m, zr_m, (peer, sub)).start()

time: 97.5 us -> 97.5 us (level)
  no operation moved by 1% of the time
where the time goes in v5:
time: 97.5 us; the launch traced here: 97.4 us
  Pallas kernels  96.7 us (99%)
    pallas_call x1, Pallas kernels, shards(): pl.pallas_call(kernel, out_shape=(jax.ShapeDtypeStruct(residual.shape, F3...  95 us

profile of v5, /device:TPU:1, one launch (start us, length us, event | category | flops | bytes accessed | tf_op | source)
XLA Modules:
  0.0 97.4 jit_solution(6892738383140281242)
XLA Ops:
  0.6 95.0 %shard_map.68 = (f32[8,4608]{1,0:T(8,128)}, f32[144,256]{1,0:T(8,128)}) custom-call(s32[1,4]{1,0:T(1,128)} %cnt_hbm.1, f32[8,4608]{1,0:T(8,128)} %res_hbm.1, s32[36,4,2304]{2,1,0:T(4,128)} %bitcast.6, f32[144,2304]{1,0:T(8,128)} %bitcast.7, f32[144,144]{1,0:T(8,128)} %bitcast.8), custom_call_target="tpu_custom_call" | custom-call | tf_op jit(solution)/shard_map/pallas_call | solution.py:652
  95.7 1.7 %shard_map.69 = (f32[8,4608]{1,0:T(8,128)}, f32[144,256]{1,0:T(8,128)}) custom-call(f32[8,4608]{1,0:T(8,128)} %get-tuple-element.6.corr_in, f32[144,256]{1,0:T(8,128)} %get-tuple-element.7.resid_in), custom_call_target="tpu_custom_call" | custom-call | tf_op jit(solution)/shard_map/pallas_call | solution.py:665
